TPU v7x, 32 devices: a whole 2x2x4 slice. The times are simulated.
32 devices in a mesh: dp: 2 (over x), tp: 4 (over z), sp: 4 (over y, core).
Axes of the slice: x: 2, y: 2, z: 4, core: 2. Of those that a mesh axis runs over, the one named last changes fastest.
Arguments:
- step_emb: bfloat16 [4, 32, 2048], P(None, 'dp'), parts along dimension 1
- v_cache: bfloat16 [2, 32, 1024, 2048], P(None, 'dp', 'sp', 'tp'), parts along dimension 1
- z_cache: bfloat16 [2, 32, 1024, 2048], P(None, 'dp', 'sp', 'tp'), parts along dimension 1
- short_state: bfloat16 [2, 32, 2, 3, 2048], P(None, 'dp', None, None, 'tp'), parts along dimension 1
- w_in: bfloat16 [2, 2048, 3, 2048], P(None, None, None, 'tp')
- b_in: float32 [2, 3, 2048], P(None, None, 'tp')
- short_taps: float32 [2, 3, 3, 2048], P(None, None, None, 'tp')
- long_filt: float32 [2, 2, 1024, 2048], P(None, None, None, 'tp')
- skip_gain: float32 [2, 2, 2048], P(None, None, 'tp')
- w_out: bfloat16 [2, 2048, 2048], P(None, 'tp')
- b_out: float32 [2, 2048], replicated
- w_up: bfloat16 [2, 2048, 8192], P(None, None, 'tp')
- w_down: bfloat16 [2, 8192, 2048], P(None, 'tp')
Outputs:
- output 1: float32 [4, 32, 2048], P(None, 'dp'), parts along dimension 1
- output 2: bfloat16 [2, 32, 1024, 2048], P(None, 'dp', 'sp', 'tp'), parts along dimension 1
- output 3: bfloat16 [2, 32, 1024, 2048], P(None, 'dp', 'sp', 'tp'), parts along dimension 1
- output 4: bfloat16 [2, 32, 2, 3, 2048], P(None, 'dp', None, None, 'tp'), parts along dimension 1
There are 2 independent parts. A program takes and returns all parts, laid end to end along the dimension named above; an argument that names none is the same for every part.
All inputs are finite; a program needn't handle non-finite values.
Results may differ from a plain program's by a relative error of at most 0.0113581.
Values sent between devices are 32-bit elements.
A program may use at most 1 GiB of HBM per device.

v0:
```python
import jax
import jax.numpy as jnp
from jax import lax
from jax.sharding import PartitionSpec as P

NUM_STEPS = 4
NUM_LAYERS = 2


def layer_norm(rows_in):
    mean_val = jnp.mean(rows_in, axis=-1, keepdims=True)
    centered = rows_in - mean_val
    var_val = jnp.mean(centered * centered, axis=-1, keepdims=True)
    return centered * lax.rsqrt(var_val + 1e-5)


def filter_windows(long_filt, shard_start, start_pos, shard_len):
    lag_pos = start_pos + 3 - shard_start - jnp.arange(shard_len + 3)
    picked = jnp.take(long_filt, jnp.maximum(lag_pos, 0), axis=2)
    return jnp.where((lag_pos >= 0)[:, None], picked, 0.0)


def append_row(cache_all, layer_idx, new_row, local_pos):
    num_seq = cache_all.shape[1]
    shard_len = cache_all.shape[2]
    chan_dim = cache_all.shape[3]
    inside = (local_pos >= 0) & (local_pos < shard_len)
    row_slot = jnp.clip(local_pos, 0, shard_len - 1)
    old_row = lax.dynamic_slice(cache_all, (layer_idx, 0, row_slot, 0), (1, num_seq, 1, chan_dim))
    put_row = jnp.where(inside, new_row[None, :, None, :], old_row)
    return lax.dynamic_update_slice(cache_all, put_row, (layer_idx, 0, row_slot, 0))


def solution(mesh):
    sp_size = mesh.shape["sp"]

    def device_fn(step_emb, v_cache, z_cache, short_state, w_in, b_in, short_taps, long_filt, skip_gain, w_out, b_out, w_up, w_down):
        shard_len = v_cache.shape[2]
        start_pos = shard_len * sp_size * 3 // 4
        shard_start = lax.axis_index("sp") * shard_len
        windows = filter_windows(long_filt, shard_start, start_pos, shard_len)
        v_all = v_cache
        z_all = z_cache
        states = [short_state[layer_idx] for layer_idx in range(NUM_LAYERS)]
        hidden_rows = []
        for step_idx in range(NUM_STEPS):
            local_pos = start_pos + step_idx - shard_start
            win_start = 3 - step_idx
            hidden = step_emb[step_idx].astype(jnp.float32)
            for layer_idx in range(NUM_LAYERS):
                normed = layer_norm(hidden).astype(jnp.bfloat16)
                proj_row = jnp.einsum("bd,dgc->bgc", normed, w_in[layer_idx], preferred_element_type=jnp.float32)
                proj_row = (proj_row + b_in[layer_idx]).astype(jnp.bfloat16)
                prev_state = states[layer_idx]
                tap_rows = short_taps[layer_idx]
                mixed_rows = (tap_rows[0] * proj_row.astype(jnp.float32)
                              + tap_rows[1] * prev_state[:, 1].astype(jnp.float32)
                              + tap_rows[2] * prev_state[:, 0].astype(jnp.float32))
                states[layer_idx] = jnp.stack([prev_state[:, 1], proj_row], axis=1)
                value_row = mixed_rows[:, 2].astype(jnp.bfloat16)
                v_all = append_row(v_all, layer_idx, value_row, local_pos)
                part_one = jnp.sum(v_all[layer_idx] * windows[layer_idx, 0, win_start:win_start + shard_len][None], axis=1)
                long_one = lax.psum(part_one, "sp") + skip_gain[layer_idx, 0] * value_row.astype(jnp.float32)
                z_row = (mixed_rows[:, 0] * long_one).astype(jnp.bfloat16)
                z_all = append_row(z_all, layer_idx, z_row, local_pos)
                part_two = jnp.sum(z_all[layer_idx] * windows[layer_idx, 1, win_start:win_start + shard_len][None], axis=1)
                long_two = lax.psum(part_two, "sp") + skip_gain[layer_idx, 1] * z_row.astype(jnp.float32)
                y_row = (mixed_rows[:, 1] * long_two).astype(jnp.bfloat16)
                mix_out = lax.psum(jnp.dot(y_row, w_out[layer_idx], preferred_element_type=jnp.float32), "tp")
                hidden = hidden + mix_out + b_out[layer_idx]
                inner_act = jax.nn.gelu(jnp.dot(layer_norm(hidden).astype(jnp.bfloat16), w_up[layer_idx], preferred_element_type=jnp.float32)).astype(jnp.bfloat16)
                hidden = hidden + lax.psum(jnp.dot(inner_act, w_down[layer_idx], preferred_element_type=jnp.float32), "tp")
            hidden_rows.append(hidden)
        return (jnp.stack(hidden_rows), v_all, z_all, jnp.stack(states))

    specs_in = (
        P(None, "dp", None),
        P(None, "dp", "sp", "tp"),
        P(None, "dp", "sp", "tp"),
        P(None, "dp", None, None, "tp"),
        P(None, None, None, "tp"),
        P(None, None, "tp"),
        P(None, None, None, "tp"),
        P(None, None, None, "tp"),
        P(None, None, "tp"),
        P(None, "tp", None),
        P(None, None),
        P(None, None, "tp"),
        P(None, "tp", None),
    )
    specs_out = (
        P(None, "dp", None),
        P(None, "dp", "sp", "tp"),
        P(None, "dp", "sp", "tp"),
        P(None, "dp", None, None, "tp"),
    )
    return jax.shard_map(device_fn, mesh=mesh, in_specs=specs_in, out_specs=specs_out, check_vma=False)
```

profile of v0, /device:TPU:0, one launch (start us, length us, event | category | flops | bytes accessed | tf_op | source)
XLA Modules:
  0.0 838.9 jit_solution(5761247696426431245)
XLA Ops:
  15.5 11.4 %copy.28 = bf16[2,16,256,512]{3,1,2,0:T(8,128)(2,1)} copy(bf16[2,16,256,512]{3,2,1,0:T(8,128)(2,1)} %param.14) | data formatting | bytes 16777216 | tf_op args[1]
  26.9 13.8 %gather_fusion = f32[259,2,2,512]{3,0,2,1:T(8,128)S(1)} fusion(f32[2,2,1024,512]{3,2,1,0:T(8,128)} %param.20, s32[1024]{0:T(1024)S(1)} %pad_clamp_fusion), kind=kCustom, calls=%fused_computation | custom fusion | bytes 4244492 | tf_op jit(solution)/shard_map/jit(_take)/gather | solution.py:19
  50.0 3.9 fusion.15
  53.9 14.4 %psum.224 = f32[16,512]{1,0:T(8,128)} all-reduce(f32[16,512]{1,0:T(8,128)} %fusion.15), channel_id=1, replica_groups=mesh['dp'=2,'tp'=4,'sp'=4] {'sp'}, use_global_device_ids=true, to_apply=%region_3.4 | all-reduce | flops 8192 | bytes 65536 | tf_op jit(solution)/shard_map/psum | solution.py:63
  69.7 11.6 %copy.30 = bf16[2,16,256,512]{3,1,2,0:T(8,128)(2,1)} copy(bf16[2,16,256,512]{3,2,1,0:T(8,128)(2,1)} %param.15) | data formatting | bytes 16777216 | tf_op args[2]
  86.5 11.5 %psum.225 = f32[16,512]{1,0:T(8,128)} all-reduce(f32[16,512]{1,0:T(8,128)} %fusion.14), channel_id=1, replica_groups=mesh['dp'=2,'tp'=4,'sp'=4] {'sp'}, use_global_device_ids=true, to_apply=%region_5.6 | all-reduce | flops 8192 | bytes 65536 | tf_op jit(solution)/shard_map/psum | solution.py:67
  105.4 30.2 %all-reduce.21.cloned.1.call-done = f32[16,2048]{1,0:T(8,128)} async-done(((f32[16,2048]{1,0:T(8,128)}), f32[16,2048]{1,0:T(8,128)}) %all-reduce.21.cloned.1.call-update) | async-done | bytes 131088 | tf_op jit(solution)/shard_map/psum | solution.py:69
  139.3 8.8 %fusion.38 = f32[16,2048]{1,0:T(8,128)} fusion(bf16[2,2048,2048]{2,1,0:T(8,128)(2,1)} %param.25, bf16[2,2048,2048]{2,1,0:T(8,128)(2,1)} %param.24, f32[16]{0:T(128)} %add_rsqrt_fusion.14, f32[16]{0:T(128)} %copy-done.37, f32[16,2048]{1,0:T(8,128)} %all-reduce.21.cloned.1.call-done, f32[2048]{0:T(1024)S(1)} %bitcast.706, bf16[4,16,2048]{2,1,0:T(8,128)(2,1)S(1)} %copy-done), kind=kOutput, calls=%fused_computation.55 | convolution fusion | flops 268926976 | bytes 17114112 | tf_op jit(solution)/shard_map/dot_general | solution.py:72
  149.0 4.4 fusion.322
  153.5 29.1 %all-reduce.23.cloned.1.call-done = f32[16,2048]{1,0:T(8,128)} async-done(((f32[16,2048]{1,0:T(8,128)}), f32[16,2048]{1,0:T(8,128)}) %all-reduce.23.cloned.1.call-update) | async-done | bytes 131088 | tf_op jit(solution)/shard_map/psum | solution.py:72
  183.9 4.5 fusion.324
  190.4 3.9 fusion.13
  195.6 3.9 fusion.11
  199.6 31.4 %all-reduce.43.cloned.1.call-done = (f32[16,512]{1,0:T(8,128)}, f32[16,512]{1,0:T(8,128)}) async-done(((f32[16,512]{1,0:T(8,128)}, f32[16,512]{1,0:T(8,128)}), (f32[16,512]{1,0:T(8,128)}, f32[16,512]{1,0:T(8,128)})) %all-reduce.43.cloned.1.call-update) | async-done | bytes 65552 | tf_op jit(solution)/shard_map/psum | solution.py:63
  232.4 3.9 fusion.12
  237.7 3.9 fusion.10
  241.5 11.5 %psum.233 = f32[16,512]{1,0:T(8,128)} all-reduce(f32[16,512]{1,0:T(8,128)} %fusion.10), channel_id=1, replica_groups=mesh['dp'=2,'tp'=4,'sp'=4] {'sp'}, use_global_device_ids=true, to_apply=%region_25.26 | all-reduce | flops 8192 | bytes 65536 | tf_op jit(solution)/shard_map/psum | solution.py:67
  257.0 33.5 %all-reduce.25.cloned.1.call-done = f32[16,2048]{1,0:T(8,128)} async-done(((f32[16,2048]{1,0:T(8,128)}), f32[16,2048]{1,0:T(8,128)}) %all-reduce.25.cloned.1.call-update) | async-done | bytes 131088 | tf_op jit(solution)/shard_map/psum | solution.py:69
  294.3 8.8 %fusion.36 = f32[16,2048]{1,0:T(8,128)} fusion(bf16[2,2048,2048]{2,1,0:T(8,128)(2,1)} %param.25, bf16[2,2048,2048]{2,1,0:T(8,128)(2,1)} %param.24, f32[16]{0:T(128)} %add_rsqrt_fusion.10, f32[16]{0:T(128)} %copy-done.38, f32[16,2048]{1,0:T(8,128)} %all-reduce.25.cloned.1.call-done, f32[2048]{0:T(1024)S(1)} %bitcast.710, bf16[4,16,2048]{2,1,0:T(8,128)(2,1)S(1)} %copy-done), kind=kOutput, calls=%fused_computation.53 | convolution fusion | flops 268926976 | bytes 17114112 | tf_op jit(solution)/shard_map/dot_general | solution.py:72
  304.2 4.4 fusion.313
  308.7 28.8 %all-reduce.27.cloned.1.call-done = f32[16,2048]{1,0:T(8,128)} async-done(((f32[16,2048]{1,0:T(8,128)}), f32[16,2048]{1,0:T(8,128)}) %all-reduce.27.cloned.1.call-update) | async-done | bytes 131088 | tf_op jit(solution)/shard_map/psum | solution.py:72
  339.3 4.5 fusion.325
  345.7 3.9 fusion.9
  351.0 3.9 fusion.7
  355.0 31.4 %all-reduce.41.cloned.1.call-done = (f32[16,512]{1,0:T(8,128)}, f32[16,512]{1,0:T(8,128)}) async-done(((f32[16,512]{1,0:T(8,128)}, f32[16,512]{1,0:T(8,128)}), (f32[16,512]{1,0:T(8,128)}, f32[16,512]{1,0:T(8,128)})) %all-reduce.41.cloned.1.call-update) | async-done | bytes 65552 | tf_op jit(solution)/shard_map/psum | solution.py:63
  387.8 3.9 fusion.8
  393.1 3.9 fusion.6
  396.9 11.5 %psum.241 = f32[16,512]{1,0:T(8,128)} all-reduce(f32[16,512]{1,0:T(8,128)} %fusion.6), channel_id=1, replica_groups=mesh['dp'=2,'tp'=4,'sp'=4] {'sp'}, use_global_device_ids=true, to_apply=%region_45.46 | all-reduce | flops 8192 | bytes 65536 | tf_op jit(solution)/shard_map/psum | solution.py:67
  411.2 34.7 %all-reduce.29.cloned.1.call-done = f32[16,2048]{1,0:T(8,128)} async-done(((f32[16,2048]{1,0:T(8,128)}), f32[16,2048]{1,0:T(8,128)}) %all-reduce.29.cloned.1.call-update) | async-done | bytes 131088 | tf_op jit(solution)/shard_map/psum | solution.py:69
  449.7 8.8 %fusion.34 = f32[16,2048]{1,0:T(8,128)} fusion(bf16[2,2048,2048]{2,1,0:T(8,128)(2,1)} %param.25, bf16[2,2048,2048]{2,1,0:T(8,128)(2,1)} %param.24, f32[16]{0:T(128)} %add_rsqrt_fusion.6, f32[16]{0:T(128)} %copy-done.36, f32[16,2048]{1,0:T(8,128)} %all-reduce.29.cloned.1.call-done, f32[2048]{0:T(1024)S(1)} %bitcast.714, bf16[4,16,2048]{2,1,0:T(8,128)(2,1)S(1)} %copy-done), kind=kOutput, calls=%fused_computation.51 | convolution fusion | flops 268926976 | bytes 17114112 | tf_op jit(solution)/shard_map/dot_general | solution.py:72
  458.7 4.5 fusion.315
  463.2 29.7 %all-reduce.31.cloned.1.call-done = f32[16,2048]{1,0:T(8,128)} async-done(((f32[16,2048]{1,0:T(8,128)}), f32[16,2048]{1,0:T(8,128)}) %all-reduce.31.cloned.1.call-update) | async-done | bytes 131088 | tf_op jit(solution)/shard_map/psum | solution.py:72
  494.7 4.5 fusion.317
  510.1 31.4 %all-reduce.39.cloned.1.call-done = (f32[16,512]{1,0:T(8,128)}, f32[16,512]{1,0:T(8,128)}) async-done(((f32[16,512]{1,0:T(8,128)}, f32[16,512]{1,0:T(8,128)}), (f32[16,512]{1,0:T(8,128)}, f32[16,512]{1,0:T(8,128)})) %all-reduce.39.cloned.1.call-update) | async-done | bytes 65552 | tf_op jit(solution)/shard_map/psum | solution.py:63
  551.2 10.3 %psum.249 = f32[16,512]{1,0:T(8,128)S(1)} all-reduce(f32[16,512]{1,0:T(8,128)S(1)} %fusion.2), channel_id=1, replica_groups=mesh['dp'=2,'tp'=4,'sp'=4] {'sp'}, use_global_device_ids=true, to_apply=%region_65.66 | all-reduce | flops 8192 | bytes 65536 | tf_op jit(solution)/shard_map/psum | solution.py:67
  564.2 34.7 %all-reduce.33.cloned.1.call-done = f32[16,2048]{1,0:T(8,128)} async-done(((f32[16,2048]{1,0:T(8,128)}), f32[16,2048]{1,0:T(8,128)}) %all-reduce.33.cloned.1.call-update) | async-done | bytes 131088 | tf_op jit(solution)/shard_map/psum | solution.py:69
  601.1 8.9 %fusion.32 = f32[16,2048]{1,0:T(8,128)} fusion(bf16[2,2048,2048]{2,1,0:T(8,128)(2,1)} %param.25, bf16[2,2048,2048]{2,1,0:T(8,128)(2,1)} %param.24, f32[16]{0:T(128)S(1)} %add_rsqrt_fusion.2, f32[16]{0:T(128)S(1)} %broadcast_multiply_fusion.2, f32[16,2048]{1,0:T(8,128)} %all-reduce.33.cloned.1.call-done, f32[2048]{0:T(1024)S(1)} %bitcast.718, ...), kind=kOutput, calls=%fused_computation.49 | convolution fusion | flops 268926976 | bytes 17114112 | tf_op jit(solution)/shard_map/dot_general | solution.py:72
  610.0 34.4 %all-reduce.35.cloned.1.call-done = f32[16,2048]{1,0:T(8,128)} async-done(((f32[16,2048]{1,0:T(8,128)}), f32[16,2048]{1,0:T(8,128)}) %all-reduce.35.cloned.1.call-update) | async-done | bytes 131088 | tf_op jit(solution)/shard_map/psum | solution.py:72
  654.0 10.4 %psum.252 = f32[16,512]{1,0:T(8,128)S(1)} all-reduce(f32[16,512]{1,0:T(8,128)S(1)} %fusion.1), channel_id=1, replica_groups=mesh['dp'=2,'tp'=4,'sp'=4] {'sp'}, use_global_device_ids=true, to_apply=%region_73.74 | all-reduce | flops 8192 | bytes 65536 | tf_op jit(solution)/shard_map/psum | solution.py:63
  669.6 31.9 %all-reduce.37.cloned.1.call-done = (f32[16,512]{1,0:T(8,128)}, f32[16,512]{1,0:T(8,128)}, f32[16,512]{1,0:T(8,128)}, f32[16,512]{1,0:T(8,128)}) async-done(((f32[16,512]{1,0:T(8,128)}, f32[16,512]{1,0:T(8,128)}, f32[16,512]{1,0:T(8,128)}, f32[16,512]{1,0:T(8,128)}), (f32[16,512]{1,0:T(8,128)}, f32[16,512]{1,0:T(8,128)}, f32[16,512]{1,0:T(8,128)}, f32[16,512]{1,0:T(8,128)})) %all-reduce.37.cloned.1.call-update) | async-done | bytes 131088 | tf_op jit(solution)/shard_map/psum | solution.py:67
  712.4 38.9 %all-reduce.47.cloned.1.call-done = (f32[16,2048]{1,0:T(8,128)}, f32[16,2048]{1,0:T(8,128)}, f32[16,2048]{1,0:T(8,128)}, f32[16,2048]{1,0:T(8,128)}) async-done(((f32[16,2048]{1,0:T(8,128)}, f32[16,2048]{1,0:T(8,128)}, f32[16,2048]{1,0:T(8,128)}, f32[16,2048]{1,0:T(8,128)}), (f32[16,2048]{1,0:T(8,128)}, f32[16,2048]{1,0:T(8,128)}, f32[16,2048]{1,0:T(8,128)}, ...) | async-done | bytes 524304 | tf_op jit(solution)/shard_map/psum | solution.py:69
  752.9 8.8 %fusion.22 = f32[16,2048]{1,0:T(8,128)} fusion(bf16[2,2048,2048]{2,1,0:T(8,128)(2,1)} %param.25, bf16[2,2048,2048]{2,1,0:T(8,128)(2,1)} %param.24, f32[16,2048]{1,0:T(8,128)S(1)} %get-tuple-element.41, f32[16]{0:T(128)S(1)} %add_rsqrt_fusion.12, f32[16]{0:T(128)S(1)} %broadcast_multiply_fusion.12), kind=kOutput, calls=%fused_computation.39 | convolution fusion | flops 268828672 | bytes 17039488 | tf_op jit(solution)/shard_map/dot_general | solution.py:72
  761.9 8.8 %fusion.20 = f32[16,2048]{1,0:T(8,128)} fusion(bf16[2,2048,2048]{2,1,0:T(8,128)(2,1)} %param.25, bf16[2,2048,2048]{2,1,0:T(8,128)(2,1)} %param.24, f32[16,2048]{1,0:T(8,128)S(1)} %get-tuple-element.101, f32[16]{0:T(128)S(1)} %add_rsqrt_fusion.8, f32[16]{0:T(128)S(1)} %broadcast_multiply_fusion.8), kind=kOutput, calls=%fused_computation.37 | convolution fusion | flops 268828672 | bytes 17039488 | tf_op jit(solution)/shard_map/dot_general | solution.py:72
  770.8 8.8 %fusion.18 = f32[16,2048]{1,0:T(8,128)} fusion(bf16[2,2048,2048]{2,1,0:T(8,128)(2,1)} %param.25, bf16[2,2048,2048]{2,1,0:T(8,128)(2,1)} %param.24, f32[16,2048]{1,0:T(8,128)S(1)} %get-tuple-element.103, f32[16]{0:T(128)S(1)} %add_rsqrt_fusion.4, f32[16]{0:T(128)S(1)} %broadcast_multiply_fusion.4), kind=kOutput, calls=%fused_computation.35 | convolution fusion | flops 268828672 | bytes 17039488 | tf_op jit(solution)/shard_map/dot_general | solution.py:72
  779.8 8.8 %fusion.16 = f32[16,2048]{1,0:T(8,128)} fusion(bf16[2,2048,2048]{2,1,0:T(8,128)(2,1)} %param.25, bf16[2,2048,2048]{2,1,0:T(8,128)(2,1)} %param.24, f32[16,2048]{1,0:T(8,128)S(1)} %get-tuple-element.105, f32[16]{0:T(128)S(1)} %add_rsqrt_fusion, f32[16]{0:T(128)S(1)} %broadcast_multiply_fusion), kind=kOutput, calls=%fused_computation.33 | convolution fusion | flops 268828672 | bytes 17039488 | tf_op jit(solution)/shard_map/dot_general | solution.py:72
  788.7 11.8 %copy.33 = bf16[2,16,256,512]{3,2,1,0:T(8,128)(2,1)} copy(bf16[2,16,256,512]{3,1,2,0:T(8,128)(2,1)} %get-tuple-element.48) | data formatting | bytes 16777216
  800.5 11.5 %copy.32 = bf16[2,16,256,512]{3,2,1,0:T(8,128)(2,1)} copy(bf16[2,16,256,512]{3,1,2,0:T(8,128)(2,1)} %fusion.475) | data formatting | bytes 16777216
  812.9 14.5 %all-reduce.45.cloned.1.call-done = (f32[16,2048]{1,0:T(8,128)}, f32[16,2048]{1,0:T(8,128)}, f32[16,2048]{1,0:T(8,128)}, f32[16,2048]{1,0:T(8,128)}) async-done(((f32[16,2048]{1,0:T(8,128)}, f32[16,2048]{1,0:T(8,128)}, f32[16,2048]{1,0:T(8,128)}, f32[16,2048]{1,0:T(8,128)}), (f32[16,2048]{1,0:T(8,128)}, f32[16,2048]{1,0:T(8,128)}, f32[16,2048]{1,0:T(8,128)}, ...) | async-done | bytes 524304 | tf_op jit(solution)/shard_map/psum | solution.py:72
  (218 shorter events, 128.1 us)
Async XLA Ops:
  7.2 128.5 %all-reduce.21.cloned.1.call-start = ((), (), s32[]{:S(2)}) async-start(), calls=%async_computation | async-start | bytes 262144 | tf_op jit(solution)/shard_map/psum | solution.py:69
  8.7 140.3 %copy-start.23 = (f32[1,1,3,512]{3,2,0,1:T(4,128)}, f32[1,1,3,512]{3,2,0,1:T(4,128)S(1)}, u32[]{:S(2)}) copy-start(f32[1,1,3,512]{3,2,0,1:T(4,128)S(1)} %copy.58) | copy-start | bytes 18436
  10.8 16.1 %copy-start.35 = (f32[16]{0:T(128)}, f32[16]{0:T(128)S(1)}, u32[]{:S(2)}) copy-start(f32[16]{0:T(128)S(1)} %get-tuple-element.135) | copy-start | bytes 196
  15.5 133.5 %copy-start.24 = (f32[1,3,512]{2,1,0:T(4,128)}, f32[1,3,512]{2,1,0:T(4,128)S(1)}, u32[]{:S(2)}) copy-start(f32[1,3,512]{2,1,0:T(4,128)S(1)} %copy.57) | copy-start | bytes 18436
  40.9 2.6 copy-start.15
  41.0 3.3 copy-start
  43.6 105.5 %copy-start.25 = (f32[3,512]{1,0:T(4,128)}, f32[3,512]{1,0:T(4,128)S(1)}, u32[]{:S(2)}) copy-start(f32[3,512]{1,0:T(4,128)S(1)} %get-tuple-element.130) | copy-start | bytes 18436
  43.6 105.5 %copy-start.26 = (f32[3,512]{1,0:T(4,128)}, f32[3,512]{1,0:T(4,128)S(1)}, u32[]{:S(2)}) copy-start(f32[3,512]{1,0:T(4,128)S(1)} %get-tuple-element.131) | copy-start | bytes 18436
  48.1 100.9 %copy-start.16 = (f32[16,3,512]{2,0,1:T(8,128)}, f32[16,3,512]{2,0,1:T(8,128)S(1)}, u32[]{:S(2)}) copy-start(f32[16,3,512]{2,0,1:T(8,128)S(1)} %get-tuple-element.111) | copy-start | bytes 294916
  69.6 11.6 %copy-start.31 = (f32[1,1,512]{2,1,0:T(1,128)}, f32[1,1,512]{2,1,0:T(1,128)S(1)}, u32[]{:S(2)}) copy-start(f32[1,1,512]{2,1,0:T(1,128)S(1)} %get-tuple-element.108) | copy-start | bytes 6148
  69.6 11.6 %copy-start.22 = (f32[16,3,512]{2,0,1:T(8,128)S(1)}, f32[16,3,512]{2,0,1:T(8,128)}, u32[]{:S(2)}) copy-start(f32[16,3,512]{2,0,1:T(8,128)} %copy-done.21) | copy-start | bytes 294916
  69.6 11.6 %copy-start.27 = (f32[16,512]{1,0:T(8,128)S(1)}, f32[16,512]{1,0:T(8,128)}, u32[]{:S(2)}) copy-start(f32[16,512]{1,0:T(8,128)} %psum.224) | copy-start | bytes 98308
  69.6 13.0 %copy-start.3 = (f32[256,512]{1,0:T(8,128)S(1)}, f32[256,512]{1,0:T(8,128)}, u32[]{:S(2)}) copy-start(f32[256,512]{1,0:T(8,128)} %get-tuple-element.86) | copy-start | bytes 1572868
  100.6 81.9 %all-reduce.23.cloned.1.call-start = ((), (), s32[]{:S(2)}) async-start(), calls=%async_computation.1 | async-start | bytes 262144 | tf_op jit(solution)/shard_map/psum | solution.py:72
  148.1 82.8 %all-reduce.43.cloned.1.call-start = ((), (), s32[]{:S(2)}) async-start(), calls=%async_computation.11 | async-start | bytes 131072 | tf_op jit(solution)/shard_map/psum | solution.py:63
  182.6 13.0 %copy-start.2 = (f32[256,512]{1,0:T(8,128)S(1)}, f32[256,512]{1,0:T(8,128)}, u32[]{:S(2)}) copy-start(f32[256,512]{1,0:T(8,128)} %get-tuple-element.84) | copy-start | bytes 1572868
  188.4 0.6 copy-start.10
  199.5 91.0 %all-reduce.25.cloned.1.call-start = ((), (), s32[]{:S(2)}) async-start(), calls=%async_computation.2 | async-start | bytes 262144 | tf_op jit(solution)/shard_map/psum | solution.py:69
  255.7 81.8 %all-reduce.27.cloned.1.call-start = ((), (), s32[]{:S(2)}) async-start(), calls=%async_computation.3 | async-start | bytes 262144 | tf_op jit(solution)/shard_map/psum | solution.py:72
  303.1 83.2 %all-reduce.41.cloned.1.call-start = ((), (), s32[]{:S(2)}) async-start(), calls=%async_computation.10 | async-start | bytes 131072 | tf_op jit(solution)/shard_map/psum | solution.py:63
  337.5 13.5 %copy-start.1 = (f32[256,512]{1,0:T(8,128)S(1)}, f32[256,512]{1,0:T(8,128)}, u32[]{:S(2)}) copy-start(f32[256,512]{1,0:T(8,128)} %get-tuple-element.80) | copy-start | bytes 1572868
  338.7 0.6 copy-start.4
  354.9 91.0 %all-reduce.29.cloned.1.call-start = ((), (), s32[]{:S(2)}) async-start(), calls=%async_computation.4 | async-start | bytes 262144 | tf_op jit(solution)/shard_map/psum | solution.py:69
  411.1 81.8 %all-reduce.31.cloned.1.call-start = ((), (), s32[]{:S(2)}) async-start(), calls=%async_computation.5 | async-start | bytes 262144 | tf_op jit(solution)/shard_map/psum | solution.py:72
  458.5 82.9 %all-reduce.39.cloned.1.call-start = ((), (), s32[]{:S(2)}) async-start(), calls=%async_computation.9 | async-start | bytes 131072 | tf_op jit(solution)/shard_map/psum | solution.py:63
  494.0 0.7 copy-start.6
  499.2 0.6 copy-start.12
  504.9 56.6 %copy-start.33 = (f32[1,1,512]{2,1,0:T(1,128)S(1)}, f32[1,1,512]{2,1,0:T(1,128)}, u32[]{:S(2)}) copy-start(f32[1,1,512]{2,1,0:T(1,128)} %get-tuple-element.107) | copy-start | bytes 6148
  510.0 88.9 %all-reduce.33.cloned.1.call-start = ((), (), s32[]{:S(2)}) async-start(), calls=%async_computation.6 | async-start | bytes 262144 | tf_op jit(solution)/shard_map/psum | solution.py:69
  564.1 80.3 %all-reduce.35.cloned.1.call-start = ((), (), s32[]{:S(2)}) async-start(), calls=%async_computation.7 | async-start | bytes 262144 | tf_op jit(solution)/shard_map/psum | solution.py:72
  601.0 43.4 %copy-start.8 = (f32[16,2048]{1,0:T(8,128)S(1)}, f32[16,2048]{1,0:T(8,128)}, u32[]{:S(2)}) copy-start(f32[16,2048]{1,0:T(8,128)} %all-reduce.33.cloned.1.call-done) | copy-start | bytes 393220
  601.1 44.6 %copy-start.9 = (f32[16,3,512]{2,0,1:T(8,128)S(1)}, f32[16,3,512]{2,0,1:T(8,128)}, u32[]{:S(2)}) copy-start(f32[16,3,512]{2,0,1:T(8,128)} %get-tuple-element.119) | copy-start | bytes 294916
  601.1 44.6 %copy-start.14 = (bf16[16,3,512]{2,0,1:T(8,128)(2,1)S(1)}, bf16[16,3,512]{2,0,1:T(8,128)(2,1)}, u32[]{:S(2)}) copy-start(bf16[16,3,512]{2,0,1:T(8,128)(2,1)} %get-tuple-element.123) | copy-start | bytes 147460
  601.1 44.6 %copy-start.17 = (f32[1,3,512]{2,1,0:T(4,128)S(1)}, f32[1,3,512]{2,1,0:T(4,128)}, u32[]{:S(2)}) copy-start(f32[1,3,512]{2,1,0:T(4,128)} %copy.55) | copy-start | bytes 18436
  601.1 44.6 %copy-start.18 = (f32[3,512]{1,0:T(4,128)S(1)}, f32[3,512]{1,0:T(4,128)}, u32[]{:S(2)}) copy-start(f32[3,512]{1,0:T(4,128)} %get-tuple-element.128) | copy-start | bytes 18436
  601.1 44.6 %copy-start.19 = (f32[3,512]{1,0:T(4,128)S(1)}, f32[3,512]{1,0:T(4,128)}, u32[]{:S(2)}) copy-start(f32[3,512]{1,0:T(4,128)} %get-tuple-element.129) | copy-start | bytes 18436
  610.0 54.4 %copy-start.30 = (f32[1,1,512]{2,1,0:T(1,128)S(1)}, f32[1,1,512]{2,1,0:T(1,128)}, u32[]{:S(2)}) copy-start(f32[1,1,512]{2,1,0:T(1,128)} %get-tuple-element.109) | copy-start | bytes 6148
  610.0 91.5 %all-reduce.37.cloned.1.call-start = ((), (), s32[]{:S(2)}) async-start(), calls=%async_computation.8 | async-start | bytes 262144 | tf_op jit(solution)/shard_map/psum | solution.py:67
  645.5 56.0 %copy-start.28 = (bf16[16,512]{1,0:T(8,128)(2,1)S(1)}, bf16[16,512]{1,0:T(8,128)(2,1)}, u32[]{:S(2)}) copy-start(bf16[16,512]{1,0:T(8,128)(2,1)} %get-tuple-element.67) | copy-start | bytes 49156
  645.5 56.0 %copy-start.32 = (f32[1,1,512]{2,1,0:T(1,128)S(1)}, f32[1,1,512]{2,1,0:T(1,128)}, u32[]{:S(2)}) copy-start(f32[1,1,512]{2,1,0:T(1,128)} %get-tuple-element.106) | copy-start | bytes 6148
  645.7 58.4 %copy-start.29 = (bf16[16,512]{1,0:T(8,128)(2,1)S(1)}, bf16[16,512]{1,0:T(8,128)(2,1)}, u32[]{:S(2)}) copy-start(bf16[16,512]{1,0:T(8,128)(2,1)} %get-tuple-element.61) | copy-start | bytes 49156
  654.0 97.4 %copy-start.5 = (f32[16,2048]{1,0:T(8,128)S(1)}, f32[16,2048]{1,0:T(8,128)}, u32[]{:S(2)}) copy-start(f32[16,2048]{1,0:T(8,128)} %copy-done.4) | copy-start | bytes 393220
  654.0 97.4 %copy-start.7 = (f32[16,2048]{1,0:T(8,128)S(1)}, f32[16,2048]{1,0:T(8,128)}, u32[]{:S(2)}) copy-start(f32[16,2048]{1,0:T(8,128)} %copy-done.6) | copy-start | bytes 393220
  654.0 97.4 %copy-start.34 = (f32[1,2048]{1,0:T(1,128)S(1)}, f32[1,2048]{1,0:T(1,128)}, u32[]{:S(2)}) copy-start(f32[1,2048]{1,0:T(1,128)} %get-tuple-element.97) | copy-start | bytes 24580
  669.5 81.8 %all-reduce.47.cloned.1.call-start = ((), (), s32[]{:S(2)}) async-start(), calls=%async_computation.13 | async-start | bytes 1048576 | tf_op jit(solution)/shard_map/psum | solution.py:69
  712.2 115.2 %all-reduce.45.cloned.1.call-start = ((), (), s32[]{:S(2)}) async-start(), calls=%async_computation.12 | async-start | bytes 1048576 | tf_op jit(solution)/shard_map/psum | solution.py:72
  779.8 8.8 %copy-start.13 = (bf16[16,3,512]{2,0,1:T(8,128)(2,1)S(1)}, bf16[16,3,512]{2,0,1:T(8,128)(2,1)}, u32[]{:S(2)}) copy-start(bf16[16,3,512]{2,0,1:T(8,128)(2,1)} %get-tuple-element.117) | copy-start | bytes 147460
  779.8 8.8 %copy-start.20 = (bf16[16,3,512]{2,0,1:T(8,128)(2,1)S(1)}, bf16[16,3,512]{2,0,1:T(8,128)(2,1)}, u32[]{:S(2)}) copy-start(bf16[16,3,512]{2,0,1:T(8,128)(2,1)} %get-tuple-element.121) | copy-start | bytes 147460
  (5 other events, 2.8 us)
Sparse Core Ops, SparseCore 0:
  100.8 34.8 all-reduce.20
  148.3 34.2 all-reduce.22
  199.6 31.2 all-reduce.42
  255.9 34.6 all-reduce.24
  303.2 34.2 all-reduce.26
  355.0 31.2 all-reduce.40
  411.3 34.6 all-reduce.28
  458.6 34.2 all-reduce.30
  510.1 31.2 all-reduce.38
  564.3 34.5 all-reduce.32
  610.1 34.2 all-reduce.34
  669.7 31.7 all-reduce.36
  712.3 39.0 all-reduce.46
  788.8 38.5 all-reduce.44
where the time goes:
time: 850 us; the launch traced here: 839 us
  waiting for transfers between devices  435 us (51%)
  matrix products  126 us (15%)
  other arithmetic  112 us (13%)
  local copies, waits for them, and re-layouts  79.8 us (9%)
  blocking collectives  69.4 us (8%)
  between operations  14.9 us (2%)
    psum x5, waiting for transfers between devices, device_fn(): lax.psum(jnp.dot(y_row, w_out[layer_idx], preferred_element_type=jnp.floa...  172 us
    psum x5, waiting for transfers between devices, device_fn(): lax.psum(jnp.dot(inner_act, w_down[layer_idx], preferred_element_type=jnp...  136 us
    psum x3, waiting for transfers between devices, device_fn(): lax.psum(part_one, 'sp')  94.1 us
    dot_general x8, matrix products, device_fn(): jnp.dot(inner_act, w_down[layer_idx], preferred_element_type=jnp.float32)  70.3 us
    unnamed x89, local copies, waits for them, and re-layouts  55.5 us
    psum x4, blocking collectives, device_fn(): lax.psum(part_two, 'sp')  44.7 us
    dot_general x8, matrix products, device_fn(): jnp.einsum('bd,dgc->bgc', normed, w_in[layer_idx], preferred_element_type...  34.3 us
    psum x1, waiting for transfers between devices, device_fn(): lax.psum(part_two, 'sp')  31.9 us
  transfers between devices with their start and end apart: 14, of which 14 were waited for; matrix products, arithmetic and copies ran while one was open for 5% of the time, Pallas kernels for 0%

commit v1 on v0

v1 whole, which is shorter than its diff:
```python
import jax
import jax.numpy as jnp
from jax import lax
from jax.sharding import PartitionSpec as P

NUM_STEPS = 4
NUM_LAYERS = 2


def layer_norm(rows_in):
    mean_val = jnp.mean(rows_in, axis=-1, keepdims=True)
    centered = rows_in - mean_val
    var_val = jnp.mean(centered * centered, axis=-1, keepdims=True)
    return centered * lax.rsqrt(var_val + 1e-5)


def gather_rows(rows, axis, zero):
    return lax.all_gather(rows.astype(jnp.float32), "sp", axis=axis, tiled=True) + zero


def solution(mesh):
    sp_size = mesh.shape["sp"]

    def device_fn(step_emb, v_cache, z_cache, short_state, w_in, b_in, short_taps, long_filt, skip_gain, w_out, b_out, w_up, w_down):
        f32 = jnp.float32
        num_seq = v_cache.shape[1]
        shard_len = v_cache.shape[2]
        start_pos = shard_len * sp_size * 3 // 4
        sp_idx = lax.axis_index("sp")
        shard_start = sp_idx * shard_len
        own = num_seq // sp_size
        lag_pos = start_pos + NUM_STEPS - 1 - shard_start - jnp.arange(shard_len + 3)
        picked = jnp.take(long_filt, jnp.clip(lag_pos, 0, sp_size * shard_len - 1), axis=2)
        parts = []
        for layer_idx in range(NUM_LAYERS):
            for which, cache in ((0, v_cache), (1, z_cache)):
                rows = cache[layer_idx].astype(f32)
                parts.append(jnp.stack([
                    jnp.sum(rows * picked[layer_idx, which, 3 - j:3 - j + shard_len][None], axis=1)
                    for j in range(NUM_STEPS)]))
        part = lax.psum_scatter(jnp.stack(parts), "sp", scatter_dimension=2, tiled=True)
        part = part.reshape(NUM_LAYERS, 2, NUM_STEPS, own, -1)
        hidden = lax.dynamic_slice_in_dim(step_emb, sp_idx * own, own, axis=1).astype(f32)
        state_own = lax.dynamic_slice_in_dim(short_state, sp_idx * own, own, axis=1)
        v_rows, z_rows, p_rows = [], [], []
        for layer_idx in range(NUM_LAYERS):
            normed = layer_norm(hidden).astype(jnp.bfloat16)
            proj = jnp.einsum("jbd,dgc->jbgc", normed, w_in[layer_idx], preferred_element_type=f32)
            proj = (proj + b_in[layer_idx]).astype(jnp.bfloat16)
            p_rows.append(proj[NUM_STEPS - 2:])
            prev = jnp.moveaxis(state_own[layer_idx], 1, 0)
            ext = jnp.concatenate([prev, proj], axis=0).astype(f32)
            taps = short_taps[layer_idx]
            mixed = taps[0] * ext[2:] + taps[1] * ext[1:-1] + taps[2] * ext[:-2]

            def conv(which, new_rows):
                filt = long_filt[layer_idx, which]
                outs = []
                for j in range(NUM_STEPS):
                    acc = part[layer_idx, which, j]
                    for i in range(j + 1):
                        acc = acc + filt[j - i] * new_rows[i]
                    outs.append(acc + skip_gain[layer_idx, which] * new_rows[j])
                return jnp.stack(outs)

            v_new = mixed[:, :, 2].astype(jnp.bfloat16).astype(f32)
            z_new = (mixed[:, :, 0] * conv(0, v_new)).astype(jnp.bfloat16).astype(f32)
            y_new = (mixed[:, :, 1] * conv(1, z_new)).astype(jnp.bfloat16)
            v_rows.append(v_new)
            z_rows.append(z_new)
            hidden = hidden + lax.psum(jnp.dot(y_new, w_out[layer_idx], preferred_element_type=f32), "tp") + b_out[layer_idx]
            inner = jax.nn.gelu(jnp.dot(layer_norm(hidden).astype(jnp.bfloat16), w_up[layer_idx], preferred_element_type=f32)).astype(jnp.bfloat16)
            hidden = hidden + lax.psum(jnp.dot(inner, w_down[layer_idx], preferred_element_type=f32), "tp")
        zero = jnp.minimum(jnp.abs(b_out[0, 0]), 0.0)
        hidden_all = gather_rows(hidden, 1, zero)
        vz = gather_rows(jnp.stack([jnp.stack(v_rows), jnp.stack(z_rows)]), 3, zero)
        vz = jnp.swapaxes(vz, 2, 3).astype(jnp.bfloat16)
        p_all = gather_rows(jnp.stack(p_rows), 2, zero)
        states = jnp.swapaxes(p_all, 1, 2).astype(jnp.bfloat16)
        last = sp_idx * shard_len == start_pos

        def put(cache, new):
            old = cache[:, :, :NUM_STEPS]
            return lax.dynamic_update_slice(cache, jnp.where(last, new, old), (0, 0, 0, 0))

        return (hidden_all, put(v_cache, vz[0]), put(z_cache, vz[1]), states)

    specs_in = (
        P(None, "dp", None),
        P(None, "dp", "sp", "tp"),
        P(None, "dp", "sp", "tp"),
        P(None, "dp", None, None, "tp"),
        P(None, None, None, "tp"),
        P(None, None, "tp"),
        P(None, None, None, "tp"),
        P(None, None, None, "tp"),
        P(None, None, "tp"),
        P(None, "tp", None),
        P(None, None),
        P(None, None, "tp"),
        P(None, "tp", None),
    )
    specs_out = (
        P(None, "dp", None),
        P(None, "dp", "sp", "tp"),
        P(None, "dp", "sp", "tp"),
        P(None, "dp", None, None, "tp"),
    )
    return jax.shard_map(device_fn, mesh=mesh, in_specs=specs_in, out_specs=specs_out, check_vma=False)
```

time: 850 us -> 287 us (0.34); the launches traced: 839 us -> 286 us
  waiting for transfers between devices: 435 us -> 154 us
  matrix products: 126 us -> 29.5 us
  other arithmetic: 112 us -> 28.4 us
  blocking collectives: 69.4 us -> 20.9 us
  local copies, waits for them, and re-layouts: 79.8 us -> 37.7 us
    psum x14 -> x4, waiting for transfers between devices: 435 us -> 127 us  [the longest x2 68.1 us: device_fn(): lax.psum(jnp.dot(inner, w_down[layer_idx], preferred_element_type=f32), '...]
    dot_general x24 -> x6, matrix products: 126 us -> 29.5 us  [the longest x2 18.1 us: device_fn(): jnp.dot(inner, w_down[layer_idx], preferred_element_type=f32)]
    psum x6 -> x0, blocking collectives: 69.4 us -> none  [the longest x4 44.7 us: device_fn(): lax.psum(part_two, 'sp')]
    reduce_sum x16 -> x2, other arithmetic: 60 us -> 19.2 us  [device_fn(): jnp.sum(rows * picked[layer_idx, which, 3 - j:3 - j + shard_len][None], a...]
    unnamed x89 -> x31, local copies, waits for them, and re-layouts: 55.5 us -> 18.9 us
    unnamed x14 -> x6, waiting for transfers between devices: 0.23 us -> 27.3 us
    dynamic_update_slice x16 -> x0, other arithmetic: 22 us -> none  [append_row(): lax.dynamic_update_slice(cache_all, put_row, (layer_idx, 0, row_slot, 0))]
    all_gather x0 -> x3, blocking collectives: none -> 20.9 us  [gather_rows(): lax.all_gather(rows.astype(jnp.float32), 'sp', axis=axis, tiled=True) + zero]
  transfers between devices with their start and end apart: 14 -> 5, of which waited for: 14 -> 5; matrix products, arithmetic and copies ran while one was open for 5% -> 4% of each run, Pallas kernels for 0% -> 0%
where the time goes in v1:
time: 287 us; the launch traced here: 286 us
  waiting for transfers between devices  154 us (54%)
  local copies, waits for them, and re-layouts  37.7 us (13%)
  matrix products  29.5 us (10%)
  other arithmetic  28.4 us (10%)
  blocking collectives  20.9 us (7%)
  between operations  15.6 us (5%)
    psum x2, waiting for transfers between devices, device_fn(): lax.psum(jnp.dot(inner, w_down[layer_idx], preferred_element_type=f32), '...  68.1 us
    psum x2, waiting for transfers between devices, device_fn(): lax.psum(jnp.dot(y_new, w_out[layer_idx], preferred_element_type=f32), 'tp')  58.7 us
    unnamed x6, waiting for transfers between devices  27.3 us
    all_gather x3, blocking collectives, gather_rows(): lax.all_gather(rows.astype(jnp.float32), 'sp', axis=axis, tiled=True) + zero  20.9 us
    reduce_sum x2, other arithmetic, device_fn(): jnp.sum(rows * picked[layer_idx, which, 3 - j:3 - j + shard_len][None], a...  19.2 us
    unnamed x31, local copies, waits for them, and re-layouts  18.9 us
    dot_general x2, matrix products, device_fn(): jnp.dot(inner, w_down[layer_idx], preferred_element_type=f32)  18.1 us
    gather x1, local copies, waits for them, and re-layouts, device_fn(): jnp.take(long_filt, jnp.clip(lag_pos, 0, sp_size * shard_len - 1), axis=2)  13.7 us
  transfers between devices with their start and end apart: 5, of which 5 were waited for; matrix products, arithmetic and copies ran while one was open for 4% of the time, Pallas kernels for 0%

profile of v1, /device:TPU:0, one launch (start us, length us, event | category | flops | bytes accessed | tf_op | source)
XLA Modules:
  0.0 286.5 jit_solution(2038446391397266626)
XLA Ops:
  7.2 7.7 %copy.92 = bf16[2,16,256,512]{3,2,1,0:T(8,128)(2,1)} copy(bf16[2,16,256,512]{3,2,1,0:T(8,128)(2,1)} %param.15) | data formatting | bytes 16777216
  14.9 7.7 %copy.91 = bf16[2,16,256,512]{3,2,1,0:T(8,128)(2,1)} copy(bf16[2,16,256,512]{3,2,1,0:T(8,128)(2,1)} %param.14) | data formatting | bytes 16777216
  22.6 13.7 %gather_fusion = f32[259,2,2,512]{3,0,2,1:T(8,128)S(1)} fusion(f32[2,2,1024,512]{3,2,1,0:T(8,128)} %param.20, s32[1024]{0:T(1024)S(1)} %pad_clamp_fusion), kind=kCustom, calls=%fused_computation | custom fusion | bytes 4244492 | tf_op jit(solution)/shard_map/jit(_take)/gather | solution.py:33
  36.3 0.2 select_bitcast_fusion
  36.6 1.1 slice_bitcast_fusion.7
  37.6 10.7 %fusion.4 = (f32[16,512]{1,0:T(8,128)S(1)}, f32[16,512]{1,0:T(8,128)S(1)}, f32[16,512]{1,0:T(8,128)S(1)}, f32[16,512]{1,0:T(8,128)S(1)}, f32[16,512]{1,0:T(8,128...) fusion(f32[256,512]{1,0:T(8,128)S(1)} %get-tuple-element.63, ...), kind=kLoop, calls=%fused_computation.21 | loop fusion | flops 37683200 | bytes 12845056 | tf_op jit(solution)/shard_map/reduce_sum | solution.py:39
  48.4 8.6 %fusion = (f32[16,512]{1,0:T(8,128)S(1)}, f32[16,512]{1,0:T(8,128)S(1)}, f32[16,512]{1,0:T(8,128)S(1)}, f32[16,512]{1,0:T(8,128)S(1)}, f32[16,512]{1,0:T(8,128)S...) fusion(f32[256,512]{1,0:T(8,128)S(1)} %get-tuple-element.67, ...), kind=kLoop, calls=%fused_computation.17 | loop fusion | flops 37683200 | bytes 12845056 | tf_op jit(solution)/shard_map/reduce_sum | solution.py:39
  57.0 0.8 pad_maximum_fusion
  57.9 0.2 all-reduce.7.cloned.1.call-start
  58.1 1.0 fusion.217
  59.2 0.1 convert_reduce_fusion
  59.3 0.2 fusion.56
  59.5 3.8 %fusion.49 = bf16[4,4,3,512]{3,1,2,0:T(4,128)(2,1)S(1)} fusion(bf16[2,2048,3,512]{3,1,2,0:T(8,128)(2,1)} %param.17, f32[4,4]{1,0:T(4,128)S(1)} %add_rsqrt_fusion.3, f32[4,4]{1,0:T(4,128)S(1)} %broadcast_multiply_fusion.3, f32[3,512]{1,0:T(4,128)S(1)} %bitcast.543, bf16[4,16,2048]{2,1,0:T(8,128)(2,1)S(1)} %copy-done.2, s32[]{:T(128)S(6)} %select_n.36), kind=kOutput, calls=%fused_computation.61 | convolution fusion | flops 100843520 | bytes 6418436 | tf_op jit(solution)/shard_map/jbd,dgc->jbgc/dot_general | solution.py:48
  63.4 0.8 constant_dynamic-slice_fusion.1
  64.5 0.5 slice.595
  65.7 0.6 dynamic-slice
  66.9 27.2 %all-reduce.15.cloned.1.call-done = f32[4,4,16,512]{3,2,1,0:T(8,128)} async-done(((f32[4,4,16,512]{3,2,1,0:T(8,128)}), f32[4,4,16,512]{3,2,1,0:T(8,128)}) %all-reduce.15.cloned.1.call-update) | async-done | bytes 524304
  94.1 1.0 constant_dynamic-slice_fusion.2
  95.2 2.7 fusion.36
  97.9 0.0 all-reduce.9.cloned.1.call-start
  97.9 34.6 %all-reduce.7.cloned.1.call-done = f32[4,4,2048]{2,1,0:T(4,128)} async-done(((f32[4,4,2048]{2,1,0:T(4,128)}), f32[4,4,2048]{2,1,0:T(4,128)}) %all-reduce.7.cloned.1.call-update) | async-done | bytes 131088 | tf_op jit(solution)/shard_map/psum | solution.py:71
  132.5 1.1 fusion.213
  133.6 1.1 multiply_reduce_fusion.2
  134.7 9.1 %fusion.20 = f32[4,4,2048]{2,1,0:T(4,128)} fusion(bf16[2,2048,2048]{2,1,0:T(8,128)(2,1)} %param.25, bf16[2,2048,2048]{2,1,0:T(8,128)(2,1)} %param.24, f32[4,4]{1,0:T(4,128)S(1)} %add_rsqrt_fusion.2, f32[4,4]{1,0:T(4,128)S(1)} %broadcast_multiply_fusion.2, f32[4,4,2048]{2,1,0:T(4,128)} %all-reduce.7.cloned.1.call-done, f32[2048]{0:T(1024)S(1)} %bitcast.515, ...), kind=kOutput, calls=%fused_computation.37 | convolution fusion | flops 268926976 | bytes 17117188 | tf_op jit(solution)/shard_map/dot_general | solution.py:73
  143.9 34.3 %all-reduce.9.cloned.1.call-done = f32[4,4,2048]{2,1,0:T(4,128)} async-done(((f32[4,4,2048]{2,1,0:T(4,128)}), f32[4,4,2048]{2,1,0:T(4,128)}) %all-reduce.9.cloned.1.call-update) | async-done | bytes 131088 | tf_op jit(solution)/shard_map/psum | solution.py:73
  178.2 1.2 fusion.215
  179.4 0.2 multiply_reduce_fusion.1
  179.6 3.8 %fusion.46 = bf16[4,4,3,512]{3,1,2,0:T(4,128)(2,1)S(1)} fusion(bf16[2,2048,3,512]{3,1,2,0:T(8,128)(2,1)} %param.17, f32[4,4,2048]{2,1,0:T(4,128)S(1)} %get-tuple-element.35, f32[4,4]{1,0:T(4,128)S(1)} %add_rsqrt_fusion.1, f32[4,4]{1,0:T(4,128)S(1)} %broadcast_multiply_fusion.1, f32[3,512]{1,0:T(4,128)S(1)} %bitcast.542), kind=kOutput, calls=%fused_computation.60 | convolution fusion | flops 100810752 | bytes 6477952 | tf_op jit(solution)/shard_map/jbd,dgc->jbgc/dot_general | solution.py:48
  183.8 0.1 copy.37
  183.9 7.2 %all_gather.10 = f32[2,2,4,16,512]{4,2,1,0,3:T(4,128)S(1)} all-gather(f32[2,2,4,4,512]{4,2,1,0,3:T(4,128)S(1)} %copy.37), channel_id=1, replica_groups=mesh['dp'=2,'tp'=4,'sp'=4] {'sp'}, dimensions={3}, use_global_device_ids=true | all-gather | bytes 655360 | tf_op jit(solution)/shard_map/all_gather | solution.py:18
  191.1 1.1 fusion.34
  192.3 0.1 copy.43
  192.3 6.6 %all_gather.11 = f32[2,2,16,3,512]{4,1,3,0,2:T(2,128)S(1)} all-gather(f32[2,2,4,3,512]{4,1,3,0,2:T(2,128)S(1)} %copy.43), channel_id=1, replica_groups=mesh['dp'=2,'tp'=4,'sp'=4] {'sp'}, dimensions={2}, use_global_device_ids=true | all-gather | bytes 491520 | tf_op jit(solution)/shard_map/all_gather | solution.py:18
  198.9 0.1 fusion.52
  199.0 0.1 fusion.53
  199.1 0.8 copy.45
  200.0 1.2 fusion.87
  201.2 0.7 copy_dynamic-update-slice_fusion
  201.9 24.1 %all-reduce.11.cloned.1.call-done = f32[4,4,2048]{2,1,0:T(4,128)} async-done(((f32[4,4,2048]{2,1,0:T(4,128)}), f32[4,4,2048]{2,1,0:T(4,128)}) %all-reduce.11.cloned.1.call-update) | async-done | bytes 131088 | tf_op jit(solution)/shard_map/psum | solution.py:71
  225.9 1.0 fusion.214
  227.0 0.2 multiply_reduce_fusion
  227.2 9.0 %fusion.16 = f32[4,4,2048]{2,1,0:T(4,128)} fusion(bf16[2,2048,2048]{2,1,0:T(8,128)(2,1)} %param.25, bf16[2,2048,2048]{2,1,0:T(8,128)(2,1)} %param.24, f32[4,4,2048]{2,1,0:T(4,128)S(1)} %get-tuple-element.33, f32[4,4]{1,0:T(4,128)S(1)} %add_rsqrt_fusion, f32[4,4]{1,0:T(4,128)S(1)} %broadcast_multiply_fusion), kind=kOutput, calls=%fused_computation.33 | convolution fusion | flops 268828672 | bytes 17039488 | tf_op jit(solution)/shard_map/dot_general | solution.py:73
  236.2 0.7 copy_dynamic-update-slice_fusion.1
  236.9 33.7 %all-reduce.13.cloned.1.call-done = f32[4,4,2048]{2,1,0:T(4,128)} async-done(((f32[4,4,2048]{2,1,0:T(4,128)}), f32[4,4,2048]{2,1,0:T(4,128)}) %all-reduce.13.cloned.1.call-update) | async-done | bytes 131088 | tf_op jit(solution)/shard_map/psum | solution.py:73
  270.6 0.9 add.473
  271.5 0.1 copy.36
  271.6 7.2 %all_gather.9 = f32[4,16,2048]{2,0,1:T(4,128)S(1)} all-gather(f32[4,4,2048]{2,0,1:T(4,128)S(1)} %copy.36), channel_id=1, replica_groups=mesh['dp'=2,'tp'=4,'sp'=4] {'sp'}, dimensions={1}, use_global_device_ids=true | all-gather | bytes 655360 | tf_op jit(solution)/shard_map/all_gather | solution.py:18
  278.8 1.1 copy.44
  (73 shorter events, 1.1 us)
Async XLA Ops:
  7.2 87.0 %all-reduce.15.cloned.1.call-start = ((), (), s32[]{:S(2)}) async-start(), calls=%async_computation.4 | async-start | bytes 1048576
  36.3 12.0 %slice-start = ((s8[8388608]{0:T(1024)(128)(4,1)}), s8[4194304]{0:T(1024)(128)(4,1)S(1)}, s32[]{:S(2)}) async-start(s8[8388608]{0:T(1024)(128)(4,1)} %bitcast.489), calls=%async_computation.5 | async-start | bytes 8388608
  36.6 11.8 %slice-start.1 = ((s8[8388608]{0:T(1024)(128)(4,1)}), s8[4194304]{0:T(1024)(128)(4,1)S(1)}, s32[]{:S(2)}) async-start(s8[8388608]{0:T(1024)(128)(4,1)} %bitcast.489), calls=%async_computation.6 | async-start | bytes 8388608
  48.3 10.8 %copy-start.2 = (bf16[4,16,2048]{2,1,0:T(8,128)(2,1)S(1)}, bf16[4,16,2048]{2,1,0:T(8,128)(2,1)}, u32[]{:S(2)}) copy-start(bf16[4,16,2048]{2,1,0:T(8,128)(2,1)} %param.13) | copy-start | bytes 786436
  48.3 11.2 %copy-start.5 = (f32[2,3,512]{2,0,1:T(2,128)S(1)}, f32[2,3,512]{2,0,1:T(2,128)}, u32[]{:S(2)}) copy-start(f32[2,3,512]{2,0,1:T(2,128)} %param.18) | copy-start | bytes 36868
  56.9 7.4 %copy-start.3 = (f32[2,3,3,512]{3,0,2,1:T(2,128)S(1)}, f32[2,3,3,512]{3,0,2,1:T(2,128)}, u32[]{:S(2)}) copy-start(f32[2,3,3,512]{3,0,2,1:T(2,128)} %param.19) | copy-start | bytes 110596
  56.9 7.4 %copy-start.4 = (f32[2,2048]{1,0:T(2,128)S(1)}, f32[2,2048]{1,0:T(2,128)}, u32[]{:S(2)}) copy-start(f32[2,2048]{1,0:T(2,128)} %param.23) | copy-start | bytes 49156
  57.0 7.5 %copy-start.6 = (f32[2,2,512]{2,1,0:T(2,128)S(1)}, f32[2,2,512]{2,1,0:T(2,128)}, u32[]{:S(2)}) copy-start(f32[2,2,512]{2,1,0:T(2,128)} %param.21) | copy-start | bytes 24580
  57.0 8.7 %copy-start.7 = (u32[32]{0:T(128)S(1)}, u32[32]{0:T(128)}, u32[]{:S(2)}) copy-start(u32[32]{0:T(128)} %constant.58) | copy-start | bytes 388
  57.9 74.6 %all-reduce.7.cloned.1.call-start = ((), (), s32[]{:S(2)}) async-start(), calls=%async_computation | async-start | bytes 262144 | tf_op jit(solution)/shard_map/psum | solution.py:71
  97.9 80.3 %all-reduce.9.cloned.1.call-start = ((), (), s32[]{:S(2)}) async-start(), calls=%async_computation.1 | async-start | bytes 262144 | tf_op jit(solution)/shard_map/psum | solution.py:73
  134.7 43.5 %copy-start.1 = (f32[4,4,2048]{2,1,0:T(4,128)S(1)}, f32[4,4,2048]{2,1,0:T(4,128)}, u32[]{:S(2)}) copy-start(f32[4,4,2048]{2,1,0:T(4,128)} %all-reduce.7.cloned.1.call-done) | copy-start | bytes 393220
  143.8 82.1 %all-reduce.11.cloned.1.call-start = ((), (), s32[]{:S(2)}) async-start(), calls=%async_computation.2 | async-start | bytes 262144 | tf_op jit(solution)/shard_map/psum | solution.py:71
  178.2 12.8 %copy-start = (bf16[2,512,2048]{2,1,0:T(8,128)(2,1)S(1)}, bf16[2,512,2048]{2,1,0:T(8,128)(2,1)}, u32[]{:S(2)}) copy-start(bf16[2,512,2048]{2,1,0:T(8,128)(2,1)} %param.22) | copy-start | bytes 12582916
  192.2 78.4 %all-reduce.13.cloned.1.call-start = ((), (), s32[]{:S(2)}) async-start(), calls=%async_computation.3 | async-start | bytes 262144 | tf_op jit(solution)/shard_map/psum | solution.py:73
Sparse Core Ops, SparseCore 0:
  58.0 36.0 all-reduce.14
  98.0 34.4 all-reduce.6
  143.9 34.2 all-reduce.8
  192.3 33.5 all-reduce.10
  236.3 34.2 all-reduce.12

commit v2 on v1

v2 whole, which is shorter than its diff:
```python
import jax
import jax.numpy as jnp
from jax import lax
from jax.experimental import pallas as pl
from jax.experimental.pallas import tpu as pltpu
from jax.sharding import PartitionSpec as P

NUM_STEPS = 4
NUM_LAYERS = 2
MESH = pl.DeviceIdType.MESH
F32 = jnp.float32
BF16 = jnp.bfloat16
VMEM_LIMIT = 66_500_000


def conv_kernel(shape, v_ref, z_ref, f_ref, vo_ref, zo_ref, part_ref, buf, fwin, fsh, rsem, wsem, fsem):
    num_seq, shard_len, chan, start_pos = shape
    half = num_seq // 2
    own = num_seq // 4
    shard_start = lax.axis_index("sp") * shard_len
    base = pl.multiple_of(jnp.maximum(start_pos - shard_len - shard_start, 0), 8)
    window = shard_len + 8

    filt_copies, reads, writes = [], [], []
    for a in range(4):
        layer, which = divmod(a, 2)
        src = (v_ref, z_ref)[which]
        dst = (vo_ref, zo_ref)[which]
        filt_copies.append(pltpu.make_async_copy(f_ref.at[layer, which, pl.ds(base, window)], fwin.at[a], fsem.at[a]))
        for c in range(2):
            reads.append(pltpu.make_async_copy(src.at[layer, pl.ds(c * half, half)], buf.at[a, c], rsem.at[a, c]))
            writes.append(pltpu.make_async_copy(buf.at[a, c], dst.at[layer, pl.ds(c * half, half)], wsem.at[a, c]))
    for a in range(4):
        filt_copies[a].start()
        reads[2 * a].start()
        reads[2 * a + 1].start()

    sub = lax.broadcasted_iota(jnp.int32, (8, chan), 0)

    def rev8(x):
        x = pltpu.roll(x, 4, 0)
        x = jnp.where((sub // 2) % 2 == 0, pltpu.roll(x, 6, 0), pltpu.roll(x, 2, 0))
        return jnp.where(sub % 2 == 0, pltpu.roll(x, 7, 0), pltpu.roll(x, 1, 0))

    groups = shard_len // 8
    for a in range(4):
        filt_copies[a].wait()

        def prep(g, prev):
            cur = rev8(fwin[a, pl.ds(pl.multiple_of((groups - 1 - g) * 8, 8), 8), :])
            for j in range(NUM_STEPS):
                mixed = jnp.where(sub >= 7 - j, prev, cur)
                fsh[j, pl.ds(pl.multiple_of(g * 8, 8), 8), :] = pltpu.roll(mixed, j + 1, 0)
            return cur

        lax.fori_loop(0, groups, prep, rev8(fwin[a, pl.ds(groups * 8, 8), :]))
        for c in range(2):
            reads[2 * a + c].wait()
            writes[2 * a + c].start()

            def lanes_body(lc, carry):
                lanes = pl.ds(pl.multiple_of(lc * 128, 128), 128)

                def body(g, accs):
                    rows = pl.ds(pl.multiple_of(g * 16, 16), 16)
                    filts = [fsh[j, rows, lanes] for j in range(NUM_STEPS)]
                    out = []
                    for b in range(half):
                        v = buf[a, c, b, rows, lanes].astype(F32)
                        for j in range(NUM_STEPS):
                            m = v * filts[j]
                            out.append(accs[b * NUM_STEPS + j] + m[:8] + m[8:])
                    return tuple(out)

                zero = jnp.zeros((8, 128), F32)
                accs = lax.fori_loop(0, shard_len // 16, body, (zero,) * (half * NUM_STEPS))
                for b in range(half):
                    for j in range(NUM_STEPS):
                        row = j * own + b % own
                        part_ref[a, c * (half // own) + b // own, row:row + 1, lanes] = jnp.sum(
                            accs[b * NUM_STEPS + j], axis=0, keepdims=True)
                return carry

            lax.fori_loop(0, chan // 128, lanes_body, 0)
    for copy in writes:
        copy.wait()


def dense_kernel(emb_ref, part_ref, state_ref, b_in_ref, taps_ref, skip_ref, b_out_ref, f_ref, w_in_ref, w_out_ref, w_up_ref, w_down_ref,
                 hid_ref, vzp_ref,
                 w_in, w_out, w_up, w_down, lags, ext, shifted, xrow, inner,
                 part_in, rs_out, rs_in, hid, fin, vzp,
                 in_sem, lag_sem, out_sem, up_sem, down_sem,
                 part_send, part_recv, rs_send, rs_recv, ag_send, ag_recv, fin_send, fin_recv, vzp_send, vzp_recv):
    t = lax.axis_index("tp")
    s = lax.axis_index("sp")
    flip_t = (3 - t, (t + 2) % 4, t + 1 - 2 * (t % 2))
    flip_s = (3 - s, (s + 2) % 4, s + 1 - 2 * (s % 2))
    rows = NUM_STEPS * 4
    cols = ext.shape[-1]
    dim = 4 * cols

    in_copies = [[pltpu.make_async_copy(w_in_ref.at[l, g], w_in.at[l, g], in_sem.at[l, g]) for g in range(3)] for l in range(2)]
    out_copies = [[pltpu.make_async_copy(w_out_ref.at[l, pl.ds(256 * i, 256)], w_out.at[l, pl.ds(256 * i, 256)], out_sem.at[l, i])
                   for i in range(cols // 256)] for l in range(2)]
    up_copies = [[pltpu.make_async_copy(w_up_ref.at[l, pl.ds(512 * i, 512)], w_up.at[l, pl.ds(512 * i, 512)], up_sem.at[l, i])
                  for i in range(4)] for l in range(2)]
    down_copies = [[pltpu.make_async_copy(w_down_ref.at[l, pl.ds(512 * i, 512)], w_down.at[l, pl.ds(512 * i, 512)], down_sem.at[l, i])
                    for i in range(4)] for l in range(2)]
    lag_copy = pltpu.make_async_copy(f_ref.at[:, :, pl.ds(0, 8)], lags, lag_sem)

    def start(copies):
        for copy in copies:
            copy.start()

    def wait(copies):
        for copy in copies:
            copy.wait()

    start(in_copies[0])
    lag_copy.start()
    start(out_copies[0])

    barrier = pltpu.get_barrier_semaphore()
    for k in range(3):
        pl.semaphore_signal(barrier, inc=1, device_id={"tp": flip_t[k]}, device_id_type=MESH)
        pl.semaphore_signal(barrier, inc=1, device_id={"sp": flip_s[k]}, device_id_type=MESH)
    pl.semaphore_wait(barrier, 6)

    sends = []

    def send(src, dst, send_sem, recv_sem, device_id):
        copy = pltpu.make_async_remote_copy(src_ref=src, dst_ref=dst, send_sem=send_sem, recv_sem=recv_sem,
                                            device_id=device_id, device_id_type=MESH)
        copy.start()
        sends.append(copy)
        return copy

    part_copies = [[send(part_ref.at[a, flip_s[k]], part_in.at[a, k], part_send.at[a, k], part_recv.at[a, k], {"sp": flip_s[k]})
                    for k in range(3)] for a in range(4)]

    def norm_to_xrow(chunks):
        mean = sum(jnp.sum(c, axis=-1, keepdims=True) for c in chunks) / dim
        cent = [c - mean for c in chunks]
        var = sum(jnp.sum(c * c, axis=-1, keepdims=True) for c in cent) / dim
        scale = lax.rsqrt(var + 1e-5)
        for i, c in enumerate(cent):
            xrow[:, cols * i:cols * (i + 1)] = (c * scale).astype(BF16)

    def reduce_chunks(r, chunk_of, base_ref, bias_row):
        copies = []
        for k in range(3):
            rs_out[r, k] = chunk_of(flip_t[k])
            copies.append(send(rs_out.at[r, k], rs_in.at[r, k], rs_send.at[r, k], rs_recv.at[r, k], {"tp": flip_t[k]}))
        total = base_ref[t] + chunk_of(t)
        if bias_row is not None:
            total = total + bias_row
        for k in (2, 1, 0):
            copies[k].wait_recv()
            total = total + rs_in[r, k]
        return total

    def gather_chunks(r, total):
        hid[r, t] = total
        copies = [send(hid.at[r, t], hid.at[r, t], ag_send.at[r, k], ag_recv.at[r, k], {"tp": flip_t[k]}) for k in range(3)]
        for copy in copies:
            copy.wait_recv()

    shifted[0:rows, :] = jnp.zeros((rows, cols), F32)
    for l in range(NUM_LAYERS):
        base = emb_ref if l == 0 else hid.at[2 * l - 1]
        norm_to_xrow([base[i] for i in range(4)])
        x = xrow[...]
        for g in range(3):
            in_copies[l][g].wait()
            proj = jnp.dot(x, w_in[l, g], preferred_element_type=F32) + b_in_ref[g, l:l + 1]
            proj = proj.astype(BF16).astype(F32)
            ext[g, 0:8] = state_ref[l, g]
            ext[g, 8:24] = proj
            vzp[s, l, 8 * g:8 * g + 8] = proj[8:16]
        start(up_copies[l])
        start(down_copies[l])

        def mixed(g):
            return (taps_ref[0, g, l:l + 1] * ext[g, 8:24] + taps_ref[1, g, l:l + 1] * ext[g, 4:20]
                    + taps_ref[2, g, l:l + 1] * ext[g, 0:16])

        def conv(which, new):
            a = 2 * l + which
            if a == 0:
                lag_copy.wait()
            shifted[rows:2 * rows, :] = new
            acc = skip_ref[l, which:which + 1] * new
            for d in range(NUM_STEPS):
                acc = acc + lags[l, which, d:d + 1] * shifted[rows - 4 * d:2 * rows - 4 * d]
            acc = acc + part_ref[a, s]
            for k in range(3):
                part_copies[a][k].wait_recv()
                acc = acc + part_in[a, k]
            return acc

        v_new = mixed(2).astype(BF16).astype(F32)
        vzp[s, l, 24:40] = v_new
        z_new = (mixed(0) * conv(0, v_new)).astype(BF16).astype(F32)
        vzp[s, l, 40:56] = z_new
        y = (mixed(1) * conv(1, z_new)).astype(BF16)
        wait(out_copies[l])
        total = reduce_chunks(
            2 * l, lambda c: jnp.dot(y, w_out[l, :, pl.ds(pl.multiple_of(c * cols, cols), cols)], preferred_element_type=F32),
            base, b_out_ref[l, t])
        gather_chunks(2 * l, total)
        vzp_copies = [send(vzp.at[s, l], vzp.at[s, l], vzp_send.at[l, k], vzp_recv.at[l, k], {"sp": flip_s[k]}) for k in range(3)]
        if l == 0:
            first_vzp = vzp_copies
            start(in_copies[1])
            start(out_copies[1])
        norm_to_xrow([hid[2 * l, i] for i in range(4)])
        x = xrow[...]
        wait(up_copies[l])
        for i in range(4):
            up = jnp.dot(x, w_up[l, :, cols * i:cols * (i + 1)], preferred_element_type=F32)
            inner[:, cols * i:cols * (i + 1)] = jax.nn.gelu(up).astype(BF16)
        act = inner[...]
        wait(down_copies[l])
        total = reduce_chunks(
            2 * l + 1, lambda c: jnp.dot(act, w_down[l, :, pl.ds(pl.multiple_of(c * cols, cols), cols)], preferred_element_type=F32),
            hid.at[2 * l], None)
        if l == 0:
            gather_chunks(1, total)

    fin[s, t] = total
    chunk_ids = (t,) + flip_t
    tp_copies = [send(fin.at[s, t], fin.at[s, t], ag_send.at[3, k], ag_recv.at[3, k], {"tp": flip_t[k]}) for k in range(3)]
    fin_copies = []
    for i in (0, 3, 2, 1):
        if i > 0:
            tp_copies[i - 1].wait_recv()
        for k in (2, 1, 0):
            chunk = fin.at[s, chunk_ids[i]]
            fin_copies.append(send(chunk, chunk, fin_send.at[i, k], fin_recv.at[i, k], {"sp": flip_s[k]}))
    for copy in fin_copies:
        copy.wait_recv()
    for g in range(4):
        for i in range(4):
            for j in range(NUM_STEPS):
                hid_ref[j, 4 * g:4 * g + 4, cols * i:cols * (i + 1)] = fin[g, i, 4 * j:4 * j + 4]
    for copy in first_vzp + vzp_copies:
        copy.wait_recv()
    vzp_ref[...] = vzp[...]
    for copy in sends:
        copy.wait_send()


def solution(mesh):
    sp_size = mesh.shape["sp"]

    def device_fn(step_emb, v_cache, z_cache, short_state, w_in, b_in, short_taps, long_filt, skip_gain, w_out, b_out, w_up, w_down):
        num_seq, shard_len, chan = v_cache.shape[1:]
        dim = step_emb.shape[-1]
        start_pos = shard_len * sp_size * 3 // 4
        sp_idx = lax.axis_index("sp")
        own = num_seq // sp_size
        rows = NUM_STEPS * own
        hbm = pl.BlockSpec(memory_space=pl.ANY)
        vmem = pl.BlockSpec(memory_space=pltpu.VMEM)
        sds = jax.ShapeDtypeStruct

        v_out, z_out, part = pl.pallas_call(
            lambda *refs: conv_kernel((num_seq, shard_len, chan, start_pos), *refs),
            name="conv_kernel",
            out_shape=(sds(v_cache.shape, BF16), sds(z_cache.shape, BF16), sds((4, sp_size, rows, chan), F32)),
            in_specs=[hbm] * 3,
            out_specs=(hbm, hbm, vmem),
            scratch_shapes=[
                pltpu.VMEM((4, 2, num_seq // 2, shard_len, chan), BF16),
                pltpu.VMEM((4, shard_len + 8, chan), F32),
                pltpu.VMEM((NUM_STEPS, shard_len, chan), F32),
                pltpu.SemaphoreType.DMA((4, 2)),
                pltpu.SemaphoreType.DMA((4, 2)),
                pltpu.SemaphoreType.DMA((4,)),
            ],
            compiler_params=pltpu.CompilerParams(vmem_limit_bytes=40_000_000),
        )(v_cache, z_cache, long_filt)

        emb = lax.dynamic_slice_in_dim(step_emb, sp_idx * own, own, axis=1).astype(F32)
        emb = jnp.moveaxis(emb.reshape(rows, 4, chan), 1, 0)
        state = lax.dynamic_slice_in_dim(short_state, sp_idx * own, own, axis=1).astype(F32)
        state = jnp.transpose(state, (0, 3, 2, 1, 4)).reshape(NUM_LAYERS, 3, 2 * own, chan)
        dma = pltpu.SemaphoreType.DMA
        chunk = (rows, chan)
        hidden, vzp = pl.pallas_call(
            dense_kernel,
            name="dense_kernel",
            out_shape=(sds((NUM_STEPS, num_seq, dim), F32), sds((sp_size, NUM_LAYERS, 56, chan), F32)),
            in_specs=[vmem] * 7 + [hbm] * 5,
            out_specs=(vmem, vmem),
            scratch_shapes=[
                pltpu.VMEM((2, 3, dim, chan), BF16),
                pltpu.VMEM((2, chan, dim), BF16),
                pltpu.VMEM((2, dim, w_up.shape[-1]), BF16),
                pltpu.VMEM((2, w_down.shape[1], dim), BF16),
                pltpu.VMEM((2, 2, 8, chan), F32),
                pltpu.VMEM((3, rows + 8, chan), F32),
                pltpu.VMEM((2 * rows, chan), F32),
                pltpu.VMEM((rows, dim), BF16),
                pltpu.VMEM((rows, w_up.shape[-1]), BF16),
                pltpu.VMEM((4, 3) + chunk, F32),
                pltpu.VMEM((4, 3) + chunk, F32),
                pltpu.VMEM((4, 3) + chunk, F32),
                pltpu.VMEM((3, 4) + chunk, F32),
                pltpu.VMEM((4, 4) + chunk, F32),
                pltpu.VMEM((4, 2, 56, chan), F32),
                dma((2, 3)), dma(()), dma((2, 2)), dma((2, 4)), dma((2, 4)),
                dma((4, 3)), dma((4, 3)), dma((4, 3)), dma((4, 3)), dma((4, 3)), dma((4, 3)), dma((4, 3)), dma((4, 3)),
                dma((2, 3)), dma((2, 3)),
            ],
            compiler_params=pltpu.CompilerParams(collective_id=0, has_side_effects=True, vmem_limit_bytes=VMEM_LIMIT),
        )(emb, part, state, jnp.transpose(b_in, (1, 0, 2)), jnp.transpose(short_taps, (1, 2, 0, 3)), skip_gain,
          b_out.reshape(NUM_LAYERS, 4, 1, chan), long_filt, jnp.transpose(w_in, (0, 2, 1, 3)), w_out, w_up, w_down)

        p_rows = vzp[:, :, :24].reshape(sp_size, NUM_LAYERS, 3, 2, own, chan)
        states = jnp.transpose(p_rows, (1, 0, 4, 3, 2, 5)).reshape(short_state.shape).astype(BF16)
        last = sp_idx * shard_len == start_pos

        def put(cache, new):
            new = new.reshape(sp_size, NUM_LAYERS, NUM_STEPS, own, chan)
            new = jnp.transpose(new, (1, 0, 3, 2, 4)).reshape(NUM_LAYERS, num_seq, NUM_STEPS, chan).astype(BF16)
            old = cache[:, :, :NUM_STEPS]
            return lax.dynamic_update_slice(cache, jnp.where(last, new, old), (0, 0, 0, 0))

        return (hidden, put(v_out, vzp[:, :, 24:40]), put(z_out, vzp[:, :, 40:56]), states)

    specs_in = (
        P(None, "dp", None),
        P(None, "dp", "sp", "tp"),
        P(None, "dp", "sp", "tp"),
        P(None, "dp", None, None, "tp"),
        P(None, None, None, "tp"),
        P(None, None, "tp"),
        P(None, None, None, "tp"),
        P(None, None, None, "tp"),
        P(None, None, "tp"),
        P(None, "tp", None),
        P(None, None),
        P(None, None, "tp"),
        P(None, "tp", None),
    )
    specs_out = (
        P(None, "dp", None),
        P(None, "dp", "sp", "tp"),
        P(None, "dp", "sp", "tp"),
        P(None, "dp", None, None, "tp"),
    )
    return jax.shard_map(device_fn, mesh=mesh, in_specs=specs_in, out_specs=specs_out, check_vma=False)
```

time: 287 us -> 95 us (0.33)
  waiting for transfers between devices: 154 us -> 0 us
  Pallas kernels: 0 us -> 78.9 us
  matrix products: 29.5 us -> 0 us
  local copies, waits for them, and re-layouts: 37.7 us -> 10 us
  other arithmetic: 28.4 us -> 4.89 us
  blocking collectives: 20.9 us -> 0 us
  between operations: 15.6 us -> 0.74 us
    psum x4 -> x0, waiting for transfers between devices: 127 us -> none  [the longest x2 68.1 us: device_fn(): lax.psum(jnp.dot(inner, w_down[layer_idx], preferred_element_type=f32), '...]
    pallas_call x0 -> x2, Pallas kernels: none -> 78.9 us  [the longest x1 58.5 us: device_fn(): pl.pallas_call(dense_kernel, name='dense_kernel', out_shape=(sds((NUM_STE...]
    dot_general x6 -> x0, matrix products: 29.5 us -> none  [the longest x2 18.1 us: device_fn(): jnp.dot(inner, w_down[layer_idx], preferred_element_type=f32)]
    unnamed x6 -> x0, waiting for transfers between devices: 27.3 us -> none
    reduce_sum x10 -> x0, other arithmetic: 24.3 us -> none  [the longest x2 19.2 us: device_fn(): jnp.sum(rows * picked[layer_idx, which, 3 - j:3 - j + shard_len][None], a...]
    all_gather x3 -> x0, blocking collectives: 20.9 us -> none  [gather_rows(): lax.all_gather(rows.astype(jnp.float32), 'sp', axis=axis, tiled=True) + zero]
    gather x1 -> x0, local copies, waits for them, and re-layouts: 13.7 us -> none  [device_fn(): jnp.take(long_filt, jnp.clip(lag_pos, 0, sp_size * shard_len - 1), axis=2)]
    unnamed x31 -> x5, local copies, waits for them, and re-layouts: 18.9 us -> 6.04 us
  transfers between devices with their start and end apart: 5 -> 0, of which waited for: 5 -> 0; matrix products, arithmetic and copies ran while one was open for 4% -> 0% of each run, Pallas kernels for 0% -> 0%
where the time goes in v2:
time: 95 us; the launch traced here: 94.6 us
  Pallas kernels  78.9 us (83%)
  local copies, waits for them, and re-layouts  10 us (11%)
  other arithmetic  4.89 us (5%)
    pallas_call x1, Pallas kernels, device_fn(): pl.pallas_call(dense_kernel, name='dense_kernel', out_shape=(sds((NUM_STE...  58.5 us
    pallas_call x1, Pallas kernels, device_fn(): pl.pallas_call(lambda *refs: conv_kernel((num_seq, shard_len, chan, start...  20.5 us
    unnamed x5, local copies, waits for them, and re-layouts  6.04 us

profile of v2, /device:TPU:0, one launch (start us, length us, event | category | flops | bytes accessed | tf_op | source)
XLA Modules:
  0.0 94.6 jit_solution(9986792514488236220)
XLA Ops:
  0.6 1.3 %reshape.35.b_out_ref = f32[2,4,1,512]{3,2,1,0:T(1,128)} reshape(f32[2,2048]{1,0:T(2,128)} %param.23) | data formatting | bytes 32768 | tf_op jit(solution)/shard_map/reshape | solution.py:319
  2.0 0.8 convert_bitcast_fusion
  2.9 0.7 reshape.37.state_ref
  3.5 0.9 dynamic-slice_convert_fusion
  4.5 0.1 reshape.38
  4.6 0.7 copy.27
  5.3 0.0 copy-start
  5.3 3.4 %copy-done = bf16[2,16,256,512]{3,2,1,0:T(8,128)(2,1)S(1)} copy-done((bf16[2,16,256,512]{3,2,1,0:T(8,128)(2,1)S(1)}, bf16[2,16,256,512]{3,2,1,0:T(8,128)(2,1)}, u32[]{:S(2)}) %copy-start) | copy-done | bytes 8388632
  8.7 20.5 %conv_kernel.1 = (bf16[2,16,256,512]{3,2,1,0:T(8,128)(2,1)}, bf16[2,16,256,512]{3,2,1,0:T(8,128)(2,1)}, f32[4,4,16,512]{3,2,1,0:T(8,128)S(1)}) custom-call(bf16[2,16,256,512]{3,2,1,0:T(8,128)(2,1)S(1)} %copy-done, bf16[2,16,256,512]{3,2,1,0:T(8,128)(2,1)} %refs_1_.1, f32[2,2,1024,512]{3,2,1,0:T(8,128)} %f_ref.1), custom_call_target="tpu_custom_call" | custom-call | tf_op jit(solution)/shard_map/conv_kernel/pallas_call | solution.py:268
  29.1 0.0 copy-start.1
  29.2 0.8 copy-done.1
  29.9 58.5 %dense_kernel.1 = (f32[4,16,2048]{2,1,0:T(8,128)}, f32[4,2,56,512]{3,2,1,0:T(8,128)}) custom-call(f32[4,16,512]{2,1,0:T(8,128)} %bitcast.22, f32[4,4,16,512]{3,2,1,0:T(8,128)} %copy-done.1, f32[2,3,8,512]{3,2,1,0:T(8,128)} %reshape.37.state_ref, f32[3,2,512]{2,1,0:T(2,128)} %bitcast.29, f32[3,3,2,512]{3,2,1,0:T(2,128)} %bitcast.28, f32[2,2,512]{2,1,0:T(2,128)} %skip_ref.1, ...), custom_call_target="tpu_custom_call" | custom-call | tf_op jit(solution)/shard_map/dense_kernel/pallas_call | solution.py:291
  88.4 1.2 %convert.9 = bf16[4,2,56,512]{3,2,1,0:T(8,128)(2,1)S(1)} convert(f32[4,2,56,512]{3,2,1,0:T(8,128)} %get-tuple-element.12) | non-fusion elementwise | flops 229376 | bytes 1376256 | tf_op jit(solution)/shard_map/convert.6
  89.8 0.1 copy.24
  89.8 0.1 convert_element_type.38
  89.9 0.8 copy.25
  90.7 0.1 copy.23
  90.8 1.9 %select_dynamic-update-slice_fusion = (bf16[2,16,256,512]{3,2,1,0:T(8,128)(2,1)}, bf16[2,16,256,512]{3,2,1,0:T(8,128)(2,1)}) fusion(bf16[2,16,256,512]{3,2,1,0:T(8,128)(2,1)} %get-tuple-element.13, bf16[2,16,4,512]{3,2,1,0:T(4,128)(2,1)S(1)} %bitcast.25, pred[]{:T(512)S(6)} %eq.3, bf16[2,16,256,512]{3,2,1,0:T(8,128)(2,1)} %get-tuple-element.11, ...), kind=kLoop, calls=%fused_computation.1 | loop fusion | flops 131072 | bytes 786433 | tf_op jit(solution)/shard_map/dynamic_update_slice | solution.py:329
  92.7 1.9 %copy.31 = f32[4,16,2048]{2,1,0:T(8,128)} copy(f32[4,16,2048]{2,1,0:T(8,128)} %get-tuple-element.22) | data formatting | bytes 1048576
  (5 shorter events, 0.1 us)
Async XLA Ops:
  5.3 3.4 %copy-start = (bf16[2,16,256,512]{3,2,1,0:T(8,128)(2,1)S(1)}, bf16[2,16,256,512]{3,2,1,0:T(8,128)(2,1)}, u32[]{:S(2)}) copy-start(bf16[2,16,256,512]{3,2,1,0:T(8,128)(2,1)} %refs_0_.1) | copy-start | bytes 25165828
  29.1 0.8 copy-start.1

commit v3 on v2

v3 whole, which is shorter than its diff:
```python
import jax
import jax.numpy as jnp
from jax import lax
from jax.experimental import pallas as pl
from jax.experimental.pallas import tpu as pltpu
from jax.sharding import PartitionSpec as P

NUM_STEPS = 4
NUM_LAYERS = 2
MESH = pl.DeviceIdType.MESH
F32 = jnp.float32
BF16 = jnp.bfloat16
VMEM_LIMIT = 66_500_000


def shift_filters(fwin, fsh):
    groups = fsh.shape[1] // 8
    sub = lax.broadcasted_iota(jnp.int32, (8, fsh.shape[2]), 0)

    def prep(g, prev):
        cur = fwin[pl.ds(pl.multiple_of((groups - 1 - g) * 8, 8), 8), :]
        for j in range(NUM_STEPS):
            mixed = jnp.where(sub <= j, prev, cur)
            fsh[j, pl.ds(pl.multiple_of(g * 8, 8), 8), :] = jnp.take_along_axis(mixed, (j - sub) % 8, axis=0)
        return cur

    lax.fori_loop(0, groups, prep, fwin[pl.ds(groups * 8, 8), :])


def conv_unit(buf, fsh, out):
    own, shard_len, chan = buf.shape

    def block_body(i, carry):
        lanes = pl.ds(pl.multiple_of(i * 128, 128), 128)
        accs = [jnp.zeros((8, 128), F32)] * (own * NUM_STEPS)
        for g in range(shard_len // 16):
            rows = pl.ds(g * 16, 16)
            filts = [fsh[j, rows, lanes] for j in range(NUM_STEPS)]
            for b in range(own):
                v = buf[b, rows, lanes].astype(F32)
                for j in range(NUM_STEPS):
                    m = v * filts[j]
                    accs[j * own + b] = accs[j * own + b] + m[:8] + m[8:]
        for row in range(own * NUM_STEPS):
            out[row:row + 1, lanes] = jnp.sum(accs[row], axis=0, keepdims=True)
        return carry

    lax.fori_loop(0, chan // 128, block_body, 0)


def window_base(shard_len):
    return pl.multiple_of(jnp.maximum((2 - lax.axis_index("sp")) * shard_len, 0), 8)


def conv_kernel(v_ref, z_ref, f_ref, vo_ref, zo_ref, part_ref, buf, fwin, fsh, rsem, wsem, fsem):
    shard_len = v_ref.shape[2]
    base = window_base(shard_len)
    filt_copies = [pltpu.make_async_copy(f_ref.at[0, a, pl.ds(base, shard_len + 8)], fwin.at[a], fsem.at[a]) for a in range(2)]
    order = []
    for i in range(8):
        order += [(0, i // 4, i % 4), (1, i // 4, i % 4)]
    reads = [pltpu.make_async_copy((v_ref, z_ref)[a].at[layer, pl.ds(4 * q, 4)], buf.at[n], rsem.at[n])
             for n, (layer, a, q) in enumerate(order)]
    writes = [pltpu.make_async_copy(buf.at[n], (vo_ref, zo_ref)[a].at[layer, pl.ds(4 * q, 4)], wsem.at[n])
              for n, (layer, a, q) in enumerate(order)]
    filt_copies[0].start()
    for n in range(4):
        reads[n].start()
    filt_copies[1].start()
    for n, (layer, a, q) in enumerate(order):
        if layer == 0 and q == 0:
            filt_copies[a].wait()
            shift_filters(fwin.at[a], fsh)
        reads[n].wait()
        writes[n].start()
        if n + 4 < 16:
            reads[n + 4].start()
        if layer == 1:
            conv_unit(buf.at[n - 1], fsh, part_ref.at[a, q])
    for copy in writes:
        copy.wait()


def dense_kernel(emb_ref, state_ref, b_in_ref, taps_ref, skip_ref, b_out_ref, part_hbm, v_ref, z_ref, f_ref, w_in_ref, w_out_ref, w_up_ref, w_down_ref,
                 fin_ref, vzp_ref,
                 w_in, w_out, w_up, w_down, lags, ext, shifted, xrow, inner, emb,
                 buf, fwin, fsh, part_ref, part_in, rs_out, rs_in, hid, fin, vzp,
                 in_sem, lag_sem, out_sem, up_sem, down_sem, own_sem, buf_sem, fwin_sem,
                 part_send, part_recv, rs_send, rs_recv, ag_send, ag_recv, fin_send, fin_recv, vzp_send, vzp_recv):
    t = lax.axis_index("tp")
    s = lax.axis_index("sp")
    flip_t = (3 - t, (t + 2) % 4, t + 1 - 2 * (t % 2))
    flip_s = (3 - s, (s + 2) % 4, s + 1 - 2 * (s % 2))
    rows = NUM_STEPS * 4
    cols = ext.shape[-1]
    dim = 4 * cols

    in_copies = [[pltpu.make_async_copy(w_in_ref.at[l, g], w_in.at[l, g], in_sem.at[l, g]) for g in range(3)] for l in range(2)]
    out_copies = [[pltpu.make_async_copy(w_out_ref.at[l, pl.ds(256 * i, 256)], w_out.at[l, pl.ds(256 * i, 256)], out_sem.at[l, i])
                   for i in range(cols // 256)] for l in range(2)]
    up_copies = [[pltpu.make_async_copy(w_up_ref.at[l, pl.ds(512 * i, 512)], w_up.at[l, pl.ds(512 * i, 512)], up_sem.at[l, i])
                  for i in range(4)] for l in range(2)]
    down_copies = [[pltpu.make_async_copy(w_down_ref.at[l, pl.ds(512 * i, 512)], w_down.at[l, pl.ds(512 * i, 512)], down_sem.at[l, i])
                    for i in range(4)] for l in range(2)]
    lag_copy = pltpu.make_async_copy(f_ref.at[:, :, pl.ds(0, 8)], lags, lag_sem)

    def start(copies):
        for copy in copies:
            copy.start()

    def wait(copies):
        for copy in copies:
            copy.wait()

    part_copy = pltpu.make_async_copy(part_hbm, part_ref.at[pl.ds(0, 2)], own_sem)
    shard_len = v_ref.shape[2]
    fwin_copies = [pltpu.make_async_copy(f_ref.at[1, a, pl.ds(window_base(shard_len), shard_len + 8)], fwin.at[a], fwin_sem.at[a])
                   for a in range(2)]
    reads = [pltpu.make_async_copy((v_ref, z_ref)[n // 4].at[1, pl.ds(4 * (n % 4), 4)], buf.at[n % 4], buf_sem.at[n]) for n in range(8)]
    part_copy.start()
    start(in_copies[0])
    lag_copy.start()
    start(out_copies[0])

    barrier = pltpu.get_barrier_semaphore()
    for k in range(3):
        pl.semaphore_signal(barrier, inc=1, device_id={"tp": flip_t[k]}, device_id_type=MESH)
        pl.semaphore_signal(barrier, inc=1, device_id={"sp": flip_s[k]}, device_id_type=MESH)
    pl.semaphore_wait(barrier, 6)

    for k in range(4):
        @pl.when(s == k)
        def _():
            for j in range(NUM_STEPS):
                for i in range(4):
                    emb[i, 4 * j:4 * j + 4] = emb_ref[j, :, cols * i:cols * (i + 1)].astype(F32)[4 * k:4 * k + 4]

    sends = []

    def send(src, dst, send_sem, recv_sem, device_id):
        copy = pltpu.make_async_remote_copy(src_ref=src, dst_ref=dst, send_sem=send_sem, recv_sem=recv_sem,
                                            device_id=device_id, device_id_type=MESH)
        copy.start()
        sends.append(copy)
        return copy

    part_copy.wait()
    def send_part(a):
        return [send(part_ref.at[a, flip_s[k]], part_in.at[a, k], part_send.at[a, k], part_recv.at[a, k], {"sp": flip_s[k]})
                for k in range(3)]

    part_copies = [send_part(0), send_part(1), None, None]

    def cached_terms(a):
        fwin_copies[a].wait()
        shift_filters(fwin.at[a], fsh)
        for q in range(4):
            n = 4 * a + q
            reads[n].wait()
            conv_unit(buf.at[q], fsh, part_ref.at[2 + a, q])
            if n + 4 < 8:
                reads[n + 4].start()
        part_copies[2 + a] = send_part(2 + a)

    def norm_to_xrow(chunks):
        mean = sum(jnp.sum(c, axis=-1, keepdims=True) for c in chunks) / dim
        cent = [c - mean for c in chunks]
        var = sum(jnp.sum(c * c, axis=-1, keepdims=True) for c in cent) / dim
        scale = lax.rsqrt(var + 1e-5)
        for i, c in enumerate(cent):
            xrow[:, cols * i:cols * (i + 1)] = (c * scale).astype(BF16)

    def reduce_chunks(r, chunk_of, base_ref, bias_row):
        copies = []
        for k in range(3):
            rs_out[r, k] = chunk_of(flip_t[k])
            copies.append(send(rs_out.at[r, k], rs_in.at[r, k], rs_send.at[r, k], rs_recv.at[r, k], {"tp": flip_t[k]}))
        total = base_ref[t] + chunk_of(t)
        if r == 0:
            cached_terms(0)
        if bias_row is not None:
            total = total + bias_row
        for k in (2, 1, 0):
            copies[k].wait_recv()
            total = total + rs_in[r, k]
        return total

    def gather_chunks(r, total):
        hid[r, t] = total
        copies = [send(hid.at[r, t], hid.at[r, t], ag_send.at[r, k], ag_recv.at[r, k], {"tp": flip_t[k]}) for k in range(3)]
        if r == 0:
            cached_terms(1)
        for copy in copies:
            copy.wait_recv()

    shifted[0:rows, :] = jnp.zeros((rows, cols), F32)
    for l in range(NUM_LAYERS):
        base = emb if l == 0 else hid.at[2 * l - 1]
        norm_to_xrow([base[i] for i in range(4)])
        x = xrow[...]
        for g in range(3):
            in_copies[l][g].wait()
            proj = jnp.dot(x, w_in[l, g], preferred_element_type=F32) + b_in_ref[g, l:l + 1]
            proj = proj.astype(BF16).astype(F32)
            ext[g, 8:24] = proj
            for b in range(4):
                old = state_ref[l, 4 * s + b, g].astype(F32)
                ext[g, b:b + 1] = old[0:1]
                ext[g, 4 + b:5 + b] = old[1:2]
            vzp[s, l, 8 * g:8 * g + 8] = proj[8:16]
        if l == 0:
            start(fwin_copies)
            start(reads[:4])
        start(up_copies[l])
        start(down_copies[l])

        def mixed(g):
            return (taps_ref[0, g, l:l + 1] * ext[g, 8:24] + taps_ref[1, g, l:l + 1] * ext[g, 4:20]
                    + taps_ref[2, g, l:l + 1] * ext[g, 0:16])

        def conv(which, new):
            a = 2 * l + which
            if a == 0:
                lag_copy.wait()
            shifted[rows:2 * rows, :] = new
            acc = skip_ref[l, which:which + 1] * new
            for d in range(NUM_STEPS):
                acc = acc + lags[l, which, d:d + 1] * shifted[rows - 4 * d:2 * rows - 4 * d]
            acc = acc + part_ref[a, s]
            for k in range(3):
                part_copies[a][k].wait_recv()
                acc = acc + part_in[a, k]
            return acc

        v_new = mixed(2).astype(BF16).astype(F32)
        vzp[s, l, 24:40] = v_new
        z_new = (mixed(0) * conv(0, v_new)).astype(BF16).astype(F32)
        vzp[s, l, 40:56] = z_new
        y = (mixed(1) * conv(1, z_new)).astype(BF16)
        wait(out_copies[l])
        total = reduce_chunks(
            2 * l, lambda c: jnp.dot(y, w_out[l, :, pl.ds(pl.multiple_of(c * cols, cols), cols)], preferred_element_type=F32),
            base, b_out_ref[l:l + 1, pl.ds(pl.multiple_of(t * cols, cols), cols)])
        gather_chunks(2 * l, total)
        vzp_copies = [send(vzp.at[s, l], vzp.at[s, l], vzp_send.at[l, k], vzp_recv.at[l, k], {"sp": flip_s[k]}) for k in range(3)]
        if l == 0:
            first_vzp = vzp_copies
            start(in_copies[1])
            start(out_copies[1])
        norm_to_xrow([hid[2 * l, i] for i in range(4)])
        x = xrow[...]
        wait(up_copies[l])
        for i in range(4):
            up = jnp.dot(x, w_up[l, :, cols * i:cols * (i + 1)], preferred_element_type=F32)
            inner[:, cols * i:cols * (i + 1)] = jax.nn.gelu(up).astype(BF16)
        act = inner[...]
        wait(down_copies[l])
        total = reduce_chunks(
            2 * l + 1, lambda c: jnp.dot(act, w_down[l, :, pl.ds(pl.multiple_of(c * cols, cols), cols)], preferred_element_type=F32),
            hid.at[2 * l], None)
        if l == 0:
            gather_chunks(1, total)

    fin[s, t] = total
    chunk_ids = (t,) + flip_t
    tp_copies = [send(fin.at[s, t], fin.at[s, t], ag_send.at[3, k], ag_recv.at[3, k], {"tp": flip_t[k]}) for k in range(3)]
    fin_copies = []
    for i in (0, 3, 2, 1):
        if i > 0:
            tp_copies[i - 1].wait_recv()
        for k in (2, 1, 0):
            chunk = fin.at[s, chunk_ids[i]]
            fin_copies.append(send(chunk, chunk, fin_send.at[i, k], fin_recv.at[i, k], {"sp": flip_s[k]}))
    for copy in fin_copies:
        copy.wait_recv()
    fin_out = pltpu.make_async_copy(fin, fin_ref, own_sem)
    fin_out.start()
    for copy in first_vzp + vzp_copies:
        copy.wait_recv()
    vzp_out = pltpu.make_async_copy(vzp, vzp_ref, lag_sem)
    vzp_out.start()
    fin_out.wait()
    vzp_out.wait()
    for copy in sends:
        copy.wait_send()


def finish_kernel(fin_ref, vzp_ref, v_ref, z_ref, hid_ref, state_ref, vo_ref, zo_ref, new_rows, sem):
    cols = fin_ref.shape[-1]
    last = lax.axis_index("sp") == 3

    @pl.when(last)
    def _():
        new_rows[...] = jnp.zeros_like(new_rows)
        for a in range(2):
            for l in range(NUM_LAYERS):
                for g in range(4):
                    for b in range(4):
                        for j in range(NUM_STEPS):
                            row = 24 + 16 * a + 4 * j + b
                            new_rows[a, l, 4 * g + b, j:j + 1] = vzp_ref[g, l, row:row + 1].astype(BF16)
        for a, dst in enumerate((vo_ref, zo_ref)):
            pltpu.make_async_copy(new_rows.at[a], dst.at[:, :, pl.ds(0, 8)], sem.at[a]).start()

    for g in range(4):
        for i in range(4):
            for j in range(NUM_STEPS):
                hid_ref[j, 4 * g:4 * g + 4, cols * i:cols * (i + 1)] = fin_ref[g, i, 4 * j:4 * j + 4]
        for l in range(NUM_LAYERS):
            for c in range(3):
                for b in range(4):
                    pair = jnp.concatenate([vzp_ref[g, l, 8 * c + b:8 * c + b + 1], vzp_ref[g, l, 8 * c + 4 + b:8 * c + 5 + b]], axis=0)
                    state_ref[l, 4 * g + b, c] = pair.astype(BF16)

    @pl.when(last)
    def _():
        for a, dst in enumerate((vo_ref, zo_ref)):
            pltpu.make_async_copy(new_rows.at[a], dst.at[:, :, pl.ds(0, 8)], sem.at[a]).wait()


def solution(mesh):
    sp_size = mesh.shape["sp"]

    def device_fn(step_emb, v_cache, z_cache, short_state, w_in, b_in, short_taps, long_filt, skip_gain, w_out, b_out, w_up, w_down):
        num_seq, shard_len, chan = v_cache.shape[1:]
        dim = step_emb.shape[-1]
        own = num_seq // sp_size
        rows = NUM_STEPS * own
        hbm = pl.BlockSpec(memory_space=pl.ANY)
        vmem = pl.BlockSpec(memory_space=pltpu.VMEM)
        sds = jax.ShapeDtypeStruct

        v_out, z_out, part = pl.pallas_call(
            conv_kernel,
            name="conv_kernel",
            out_shape=(sds(v_cache.shape, BF16), sds(z_cache.shape, BF16), sds((2, sp_size, rows, chan), F32)),
            in_specs=[hbm] * 3,
            out_specs=(hbm, hbm, vmem),
            scratch_shapes=[
                pltpu.VMEM((16, own, shard_len, chan), BF16),
                pltpu.VMEM((2, shard_len + 8, chan), F32),
                pltpu.VMEM((NUM_STEPS, shard_len, chan), F32),
                pltpu.SemaphoreType.DMA((16,)),
                pltpu.SemaphoreType.DMA((16,)),
                pltpu.SemaphoreType.DMA((2,)),
            ],
            compiler_params=pltpu.CompilerParams(vmem_limit_bytes=VMEM_LIMIT),
        )(v_cache, z_cache, long_filt)

        dma = pltpu.SemaphoreType.DMA
        chunk = (rows, chan)
        fin, vzp = pl.pallas_call(
            dense_kernel,
            name="dense_kernel",
            out_shape=(sds((sp_size, 4) + chunk, F32), sds((sp_size, NUM_LAYERS, 56, chan), F32)),
            in_specs=[vmem] * 6 + [hbm] * 8,
            out_specs=(hbm, hbm),
            scratch_shapes=[
                pltpu.VMEM((2, 3, dim, chan), BF16),
                pltpu.VMEM((2, chan, dim), BF16),
                pltpu.VMEM((2, dim, w_up.shape[-1]), BF16),
                pltpu.VMEM((2, w_down.shape[1], dim), BF16),
                pltpu.VMEM((2, 2, 8, chan), F32),
                pltpu.VMEM((3, rows + 8, chan), F32),
                pltpu.VMEM((2 * rows, chan), F32),
                pltpu.VMEM((rows, dim), BF16),
                pltpu.VMEM((rows, w_up.shape[-1]), BF16),
                pltpu.VMEM((4,) + chunk, F32),
                pltpu.VMEM((4, own, shard_len, chan), BF16),
                pltpu.VMEM((2, shard_len + 8, chan), F32),
                pltpu.VMEM((NUM_STEPS, shard_len, chan), F32),
                pltpu.VMEM((4, 4) + chunk, F32),
                pltpu.VMEM((4, 3) + chunk, F32),
                pltpu.VMEM((4, 3) + chunk, F32),
                pltpu.VMEM((4, 3) + chunk, F32),
                pltpu.VMEM((3, 4) + chunk, F32),
                pltpu.VMEM((4, 4) + chunk, F32),
                pltpu.VMEM((4, 2, 56, chan), F32),
                dma((2, 3)), dma(()), dma((2, 2)), dma((2, 4)), dma((2, 4)), dma(()), dma((8,)), dma((2,)),
                dma((4, 3)), dma((4, 3)), dma((4, 3)), dma((4, 3)), dma((4, 3)), dma((4, 3)), dma((4, 3)), dma((4, 3)),
                dma((2, 3)), dma((2, 3)),
            ],
            compiler_params=pltpu.CompilerParams(collective_id=0, has_side_effects=True, vmem_limit_bytes=VMEM_LIMIT),
        )(step_emb, jnp.transpose(short_state, (0, 1, 3, 2, 4)), jnp.transpose(b_in, (1, 0, 2)), jnp.transpose(short_taps, (1, 2, 0, 3)),
          skip_gain, b_out, part, v_cache, z_cache, long_filt, jnp.transpose(w_in, (0, 2, 1, 3)), w_out, w_up, w_down)

        hidden, states, v_out, z_out = pl.pallas_call(
            finish_kernel,
            name="finish_kernel",
            out_shape=(sds((NUM_STEPS, num_seq, dim), F32), sds((NUM_LAYERS, num_seq, 3, 2, chan), BF16),
                       sds(v_cache.shape, BF16), sds(z_cache.shape, BF16)),
            in_specs=[vmem, vmem, hbm, hbm],
            out_specs=(vmem, vmem, hbm, hbm),
            input_output_aliases={2: 2, 3: 3},
            scratch_shapes=[pltpu.VMEM((2, NUM_LAYERS, num_seq, 8, chan), BF16), dma((2,))],
            compiler_params=pltpu.CompilerParams(vmem_limit_bytes=VMEM_LIMIT),
        )(fin, vzp, v_out, z_out)
        return (hidden, v_out, z_out, jnp.transpose(states, (0, 1, 3, 2, 4)))

    specs_in = (
        P(None, "dp", None),
        P(None, "dp", "sp", "tp"),
        P(None, "dp", "sp", "tp"),
        P(None, "dp", None, None, "tp"),
        P(None, None, None, "tp"),
        P(None, None, "tp"),
        P(None, None, None, "tp"),
        P(None, None, None, "tp"),
        P(None, None, "tp"),
        P(None, "tp", None),
        P(None, None),
        P(None, None, "tp"),
        P(None, "tp", None),
    )
    specs_out = (
        P(None, "dp", None),
        P(None, "dp", "sp", "tp"),
        P(None, "dp", "sp", "tp"),
        P(None, "dp", None, None, "tp"),
    )
    return jax.shard_map(device_fn, mesh=mesh, in_specs=specs_in, out_specs=specs_out, check_vma=False)
```

time: 95 us -> 75.4 us (0.79)
  local copies, waits for them, and re-layouts: 10 us -> 0 us
  other arithmetic: 4.89 us -> 0 us
  Pallas kernels: 78.9 us -> 74.6 us
    unnamed x5 -> x0, local copies, waits for them, and re-layouts: 6.04 us -> none
    pallas_call x2 -> x3, Pallas kernels: 78.9 us -> 74.6 us  [the longest x1 57.4 us: device_fn(): pl.pallas_call(dense_kernel, name='dense_kernel', out_shape=(sds((sp_size...]
    reshape x3 -> x0, local copies, waits for them, and re-layouts: 2.05 us -> none  [the longest x1 1.35 us: device_fn(): b_out.reshape(NUM_LAYERS, 4, 1, chan)]
    dynamic_update_slice x1 -> x0, other arithmetic: 1.89 us -> none  [put(): lax.dynamic_update_slice(cache, jnp.where(last, new, old), (0, 0, 0, 0))]
    another operation x1 -> x0, other arithmetic: 1.24 us -> none
    convert_element_type x6 -> x0, local copies, waits for them, and re-layouts: 1.06 us -> none  [the longest x2 0.88 us: device_fn(): jnp.transpose(p_rows, (1, 0, 4, 3, 2, 5)).reshape(short_state.shape)]
where the time goes in v3:
time: 75.4 us; the launch traced here: 75.2 us
  Pallas kernels  74.6 us (99%)
    pallas_call x1, Pallas kernels, device_fn(): pl.pallas_call(dense_kernel, name='dense_kernel', out_shape=(sds((sp_size...  57.4 us
    pallas_call x1, Pallas kernels, device_fn(): pl.pallas_call(conv_kernel, name='conv_kernel', out_shape=(sds(v_cache.sh...  14.7 us
    pallas_call x1, Pallas kernels, device_fn(): pl.pallas_call(finish_kernel, name='finish_kernel', out_shape=(sds((NUM_S...  2.49 us

profile of v3, /device:TPU:0, one launch (start us, length us, event | category | flops | bytes accessed | tf_op | source)
XLA Modules:
  0.0 75.2 jit_solution(4400947549822224044)
XLA Ops:
  0.6 14.7 %conv_kernel.1 = (bf16[2,16,256,512]{3,2,1,0:T(8,128)(2,1)}, bf16[2,16,256,512]{3,2,1,0:T(8,128)(2,1)}, f32[2,4,16,512]{3,2,1,0:T(8,128)}) custom-call(bf16[2,16,256,512]{3,2,1,0:T(8,128)(2,1)} %v_ref.3, bf16[2,16,256,512]{3,2,1,0:T(8,128)(2,1)} %z_ref.3, f32[2,2,1024,512]{3,2,1,0:T(8,128)} %f_ref.3), custom_call_target="tpu_custom_call" | custom-call | tf_op jit(solution)/shard_map/conv_kernel/pallas_call | solution.py:333
  15.3 57.4 %dense_kernel.1 = (f32[4,4,16,512]{3,2,1,0:T(8,128)}, f32[4,2,56,512]{3,2,1,0:T(8,128)}) custom-call(bf16[4,16,2048]{2,1,0:T(8,128)(2,1)} %emb_ref.1, bf16[2,16,3,2,512]{4,3,2,1,0:T(2,128)(2,1)} %bitcast.6, f32[3,2,512]{2,1,0:T(2,128)} %bitcast.8, f32[3,3,2,512]{3,2,1,0:T(2,128)} %bitcast.7, f32[2,2,512]{2,1,0:T(2,128)} %skip_ref.1, f32[2,2048]{1,0:T(2,128)} %b_out_ref.1, ...), custom_call_target="tpu_custom_call" | custom-call | tf_op jit(solution)/shard_map/dense_kernel/pallas_call | solution.py:352
  72.7 2.5 %finish_kernel.1 = (f32[4,16,2048]{2,1,0:T(8,128)}, bf16[2,16,3,2,512]{4,3,2,1,0:T(2,128)(2,1)}, bf16[2,16,256,512]{3,2,1,0:T(8,128)(2,1)}, bf16[2,16,256,512]{3,2,1,0:T(8,128)(2,1)}) custom-call(f32[4,4,16,512]{3,2,1,0:T(8,128)} %get-tuple-element.14.fin_ref, ...), custom_call_target="tpu_custom_call", output_to_operand_aliasing={{2}: (2, {}), {3}: (3, {})} | custom-call | tf_op jit(solution)/shard_map/finish_kernel/pallas_call | solution.py:387

commit v4 on v3

v4 whole, which is shorter than its diff:
```python
import jax
import jax.numpy as jnp
from jax import lax
from jax.experimental import pallas as pl
from jax.experimental.pallas import tpu as pltpu
from jax.sharding import PartitionSpec as P

NUM_STEPS = 4
NUM_LAYERS = 2
MESH = pl.DeviceIdType.MESH
F32 = jnp.float32
BF16 = jnp.bfloat16
VMEM_LIMIT = 66_500_000
AHEAD = 8
SUB = 1


def shift_filters(fwin, fsh):
    groups = fsh.shape[1] // 8
    sub = lax.broadcasted_iota(jnp.int32, (8, fsh.shape[2]), 0)

    def prep(g, prev):
        cur = fwin[pl.ds(pl.multiple_of((groups - 1 - g) * 8, 8), 8), :]
        for j in range(NUM_STEPS):
            mixed = jnp.where(sub <= j, prev, cur)
            fsh[j, pl.ds(pl.multiple_of(g * 8, 8), 8), :] = jnp.take_along_axis(mixed, (j - sub) % 8, axis=0)
        return cur

    lax.fori_loop(0, groups, prep, fwin[pl.ds(groups * 8, 8), :])


def conv_unit(buf, fsh, out):
    own, shard_len, chan = buf.shape

    def block_body(i, carry):
        lanes = pl.ds(pl.multiple_of(i * 128, 128), 128)
        accs = [jnp.zeros((8, 128), F32)] * (own * NUM_STEPS)
        for g in range(shard_len // 16):
            rows = pl.ds(g * 16, 16)
            filts = [fsh[j, rows, lanes] for j in range(NUM_STEPS)]
            for b in range(own):
                v = buf[b, rows, lanes].astype(F32)
                for j in range(NUM_STEPS):
                    m = v * filts[j]
                    accs[j * own + b] = accs[j * own + b] + m[:8] + m[8:]
        for row in range(own * NUM_STEPS):
            out[row:row + 1, lanes] = jnp.sum(accs[row], axis=0, keepdims=True)
        return carry

    lax.fori_loop(0, chan // 128, block_body, 0)


def window_base(shard_len):
    return pl.multiple_of(jnp.maximum((2 - lax.axis_index("sp")) * shard_len, 0), 8)


def conv_kernel(v_ref, z_ref, f_ref, vo_ref, zo_ref, part_out, buf, fwin, fsh, part_ref, rsem, wsem, fsem, psem):
    shard_len = v_ref.shape[2]
    base = window_base(shard_len)
    filt_copies = [pltpu.make_async_copy(f_ref.at[0, a, pl.ds(base, shard_len + 8)], fwin.at[a], fsem.at[a]) for a in range(2)]
    order = []
    for i in range(8):
        order += [(0, i // 4, i % 4), (1, i // 4, i % 4)]
    reads = [pltpu.make_async_copy((v_ref, z_ref)[a].at[layer, pl.ds(4 * q, 4)], buf.at[n], rsem.at[n])
             for n, (layer, a, q) in enumerate(order)]
    writes = [pltpu.make_async_copy(buf.at[n], (vo_ref, zo_ref)[a].at[layer, pl.ds(4 * q, 4)], wsem.at[n])
              for n, (layer, a, q) in enumerate(order)]
    part_copies = [pltpu.make_async_copy(part_ref.at[a], part_out.at[a], psem.at[a]) for a in range(2)]
    filt_copies[0].start()
    for n in range(AHEAD):
        reads[n].start()
    filt_copies[1].start()
    done = 0

    def pass_on(upto):
        for n in range(done, upto):
            reads[n].wait()
            writes[n].start()
            if n + AHEAD < 16:
                reads[n + AHEAD].start()

    for i in range(8):
        a, q = divmod(i, 4)
        pass_on(min(2 * i + 3, 16))
        done = min(2 * i + 3, 16)
        if q == 0:
            filt_copies[a].wait()
            shift_filters(fwin.at[a], fsh)
        conv_unit(buf.at[2 * i], fsh, part_ref.at[a, q])
        if q == 3:
            part_copies[a].start()
    for copy in writes + part_copies:
        copy.wait()


def dense_kernel(emb_hbm, state_hbm, b_in_hbm, taps_hbm, skip_hbm, b_out_hbm, part_hbm, v_ref, z_ref, f_ref, w_in_ref, w_out_ref, w_up_ref, w_down_ref,
                 hid_out, state_out, rows_out,
                 emb_ref, state_ref, b_in_ref, taps_ref, skip_ref, b_out_ref,
                 w_in, w_out, w_up, w_down, lags, ext, shifted, xrow, inner, emb,
                 buf, fwin, fsh, part_ref, part_in, rs_out, rs_in, hid, fin, vzp, hid_v, state_v, rows_v,
                 in_sem, lag_sem, out_sem, up_sem, down_sem, own_sem, buf_sem, fwin_sem, fin_sem, small_sem,
                 part_send, part_recv, rs_send, rs_recv, ag_send, ag_recv, fin_send, fin_recv, vzp_send, vzp_recv):
    t = lax.axis_index("tp")
    s = lax.axis_index("sp")
    flip_t = (3 - t, (t + 2) % 4, t + 1 - 2 * (t % 2))
    flip_s = (3 - s, (s + 2) % 4, s + 1 - 2 * (s % 2))
    middle = (t + 1) // 2 % 2
    slot_t = (middle, 1 - middle, 2)
    peer_t = (flip_t[0] + middle * (flip_t[1] - flip_t[0]), flip_t[1] + middle * (flip_t[0] - flip_t[1]), flip_t[2])
    rows = NUM_STEPS * 4
    cols = ext.shape[-1]
    dim = 4 * cols
    width = cols // SUB

    in_copies = [[pltpu.make_async_copy(w_in_ref.at[l, g], w_in.at[l, g], in_sem.at[l, g]) for g in range(3)] for l in range(2)]
    out_copies = [[pltpu.make_async_copy(w_out_ref.at[l, pl.ds(256 * i, 256)], w_out.at[l, pl.ds(256 * i, 256)], out_sem.at[l, i])
                   for i in range(cols // 256)] for l in range(2)]
    up_copies = [[pltpu.make_async_copy(w_up_ref.at[l, pl.ds(512 * i, 512)], w_up.at[l, pl.ds(512 * i, 512)], up_sem.at[l, i])
                  for i in range(4)] for l in range(2)]
    down_copies = [[pltpu.make_async_copy(w_down_ref.at[l, pl.ds(512 * i, 512)], w_down.at[l, pl.ds(512 * i, 512)], down_sem.at[l, i])
                    for i in range(4)] for l in range(2)]
    lag_copy = pltpu.make_async_copy(f_ref.at[:, :, pl.ds(0, 8)], lags, lag_sem)

    def start(copies):
        for copy in copies:
            copy.start()

    def wait(copies):
        for copy in copies:
            copy.wait()

    part_copy = pltpu.make_async_copy(part_hbm, part_ref.at[pl.ds(0, 2)], own_sem)
    shard_len = v_ref.shape[2]
    fwin_copies = [pltpu.make_async_copy(f_ref.at[1, a, pl.ds(window_base(shard_len), shard_len + 8)], fwin.at[a], fwin_sem.at[a])
                   for a in range(2)]
    reads = [pltpu.make_async_copy((v_ref, z_ref)[n // 4].at[1, pl.ds(4 * (n % 4), 4)], buf.at[n % 4], buf_sem.at[n]) for n in range(8)]
    small_copies = [pltpu.make_async_copy(src, dst, small_sem.at[i]) for i, (src, dst) in enumerate((
        (emb_hbm, emb_ref), (state_hbm, state_ref), (b_in_hbm, b_in_ref), (taps_hbm, taps_ref), (skip_hbm, skip_ref), (b_out_hbm, b_out_ref)))]
    start(small_copies)
    part_copy.start()
    start(in_copies[0])
    lag_copy.start()
    start(out_copies[0])

    barrier = pltpu.get_barrier_semaphore()
    for k in range(3):
        pl.semaphore_signal(barrier, inc=1, device_id={"tp": flip_t[k]}, device_id_type=MESH)
        pl.semaphore_signal(barrier, inc=1, device_id={"sp": flip_s[k]}, device_id_type=MESH)
    pl.semaphore_wait(barrier, 6)

    wait(small_copies)
    for k in range(4):
        @pl.when(s == k)
        def _():
            for j in range(NUM_STEPS):
                for i in range(4):
                    for u in range(SUB):
                        first = cols * i + width * u
                        emb[i, u, 4 * j:4 * j + 4] = emb_ref[j, :, first:first + width].astype(F32)[4 * k:4 * k + 4]

    sends = []

    def send(src, dst, send_sem, recv_sem, device_id):
        copy = pltpu.make_async_remote_copy(src_ref=src, dst_ref=dst, send_sem=send_sem, recv_sem=recv_sem,
                                            device_id=device_id, device_id_type=MESH)
        copy.start()
        sends.append(copy)
        return copy

    part_copy.wait()
    def send_part(a):
        return [send(part_ref.at[a, flip_s[k]], part_in.at[a, k], part_send.at[a, k], part_recv.at[a, k], {"sp": flip_s[k]})
                for k in range(3)]

    part_copies = [send_part(0), send_part(1), None, None]

    def cached_terms(a, first, count):
        if first == 0:
            fwin_copies[a].wait()
            shift_filters(fwin.at[a], fsh)
        for q in range(first, first + count):
            n = 4 * a + q
            reads[n].wait()
            conv_unit(buf.at[q], fsh, part_ref.at[2 + a, q])
            if n + 4 < 8:
                reads[n + 4].start()
        if first + count == 4:
            part_copies[2 + a] = send_part(2 + a)

    def order_rows(l):
        for copy in vzp_copies[l]:
            copy.wait_recv()
        for g in range(4):
            for c in range(3):
                for b in range(4):
                    first = 8 * c + b
                    pair = jnp.concatenate([vzp[g, l, first:first + 1], vzp[g, l, first + 4:first + 5]], axis=0)
                    state_v[l, 4 * g + b, c] = pair.astype(BF16)

        @pl.when(s == 3)
        def _():
            for a in range(2):
                for g in range(4):
                    for b in range(4):
                        first = 24 + 16 * a + b
                        new = [vzp[g, l, first + 4 * j:first + 4 * j + 1] for j in range(NUM_STEPS)]
                        new = jnp.concatenate(new + [jnp.zeros((4, cols), F32)], axis=0)
                        rows_v[a, l, 4 * g + b] = new.astype(BF16)

    def norm_to_xrow(pieces):
        mean = sum(jnp.sum(c, axis=-1, keepdims=True) for c in pieces) / dim
        cent = [c - mean for c in pieces]
        var = sum(jnp.sum(c * c, axis=-1, keepdims=True) for c in cent) / dim
        scale = lax.rsqrt(var + 1e-5)
        for i, c in enumerate(cent):
            xrow[:, width * i:width * (i + 1)] = (c * scale).astype(BF16)

    def reduce_gather(r, act, weight, base_ref, bias_of, out_ref):
        def piece(c, u):
            return jnp.dot(act, weight[:, pl.ds(pl.multiple_of(c * cols + u * width, width), width)], preferred_element_type=F32)

        copies = []
        for u in range(SUB):
            for k, peer in zip(slot_t, peer_t):
                rs_out[r, k, u] = piece(peer, u)
                copies.append(send(rs_out.at[r, k, u], rs_in.at[r, k, u], rs_send.at[r, k, u], rs_recv.at[r, k, u], {"tp": peer}))
        totals = [base_ref[t, u] + piece(t, u) for u in range(SUB)]
        if bias_of is not None:
            totals = [total + bias_of(u) for u, total in enumerate(totals)]
        if r == 0:
            cached_terms(0, 0, 3)
        if r == 1:
            cached_terms(1, 1, 3)
        if r == 2:
            order_rows(0)
        gathers = []
        for u in range(SUB):
            total = totals[u]
            for k in (2, 1, 0):
                copies[3 * u + k].wait_recv()
                total = total + rs_in[r, slot_t[k], u]
            out_ref[t, u] = total
            own = out_ref.at[t, u]
            gathers.append([send(own, own, ag_send.at[r, k, u], ag_recv.at[r, k, u], {"tp": peer}) for k, peer in zip(slot_t, peer_t)])
        if r == 0:
            cached_terms(0, 3, 1)
            cached_terms(1, 0, 1)
        return gathers

    def wait_gather(gathers):
        for copies in gathers:
            for copy in copies:
                copy.wait_recv()

    def pieces_of(ref):
        return [ref[i, u] for i in range(4) for u in range(SUB)]

    vzp_copies = []
    shifted[0:rows, :] = jnp.zeros((rows, cols), F32)
    for l in range(NUM_LAYERS):
        base = emb if l == 0 else hid.at[2 * l - 1]
        norm_to_xrow(pieces_of(base))
        x = xrow[...]
        for g in range(3):
            in_copies[l][g].wait()
            proj = jnp.dot(x, w_in[l, g], preferred_element_type=F32) + b_in_ref[g, l:l + 1]
            proj = proj.astype(BF16).astype(F32)
            ext[g, 8:24] = proj
            for b in range(4):
                old = state_ref[l, 4 * s + b, g].astype(F32)
                ext[g, b:b + 1] = old[0:1]
                ext[g, 4 + b:5 + b] = old[1:2]
            vzp[s, l, 8 * g:8 * g + 8] = proj[8:16]
        if l == 0:
            start(fwin_copies)
            start(reads[:4])
        start(up_copies[l])
        start(down_copies[l])

        def mixed(g):
            return (taps_ref[0, g, l:l + 1] * ext[g, 8:24] + taps_ref[1, g, l:l + 1] * ext[g, 4:20]
                    + taps_ref[2, g, l:l + 1] * ext[g, 0:16])

        def conv(which, new):
            a = 2 * l + which
            if a == 0:
                lag_copy.wait()
            shifted[rows:2 * rows, :] = new
            acc = skip_ref[l, which:which + 1] * new
            for d in range(NUM_STEPS):
                acc = acc + lags[l, which, d:d + 1] * shifted[rows - 4 * d:2 * rows - 4 * d]
            acc = acc + part_ref[a, s]
            for k in range(3):
                part_copies[a][k].wait_recv()
                acc = acc + part_in[a, k]
            return acc

        v_new = mixed(2).astype(BF16).astype(F32)
        vzp[s, l, 24:40] = v_new
        z_new = (mixed(0) * conv(0, v_new)).astype(BF16).astype(F32)
        vzp[s, l, 40:56] = z_new
        y = (mixed(1) * conv(1, z_new)).astype(BF16)
        wait(out_copies[l])
        bias = [b_out_ref[l:l + 1, pl.ds(pl.multiple_of(t * cols + u * width, width), width)] for u in range(SUB)]
        gathers = reduce_gather(2 * l, y, w_out.at[l], base, lambda u: bias[u], hid.at[2 * l])
        vzp_copies.append([send(vzp.at[s, l], vzp.at[s, l], vzp_send.at[l, k], vzp_recv.at[l, k], {"sp": flip_s[k]}) for k in range(3)])
        if l == 0:
            start(in_copies[1])
            start(out_copies[1])
        wait_gather(gathers)
        norm_to_xrow(pieces_of(hid.at[2 * l]))
        x = xrow[...]
        wait(up_copies[l])
        for i in range(4):
            up = jnp.dot(x, w_up[l, :, cols * i:cols * (i + 1)], preferred_element_type=F32)
            inner[:, cols * i:cols * (i + 1)] = jax.nn.gelu(up).astype(BF16)
        act = inner[...]
        wait(down_copies[l])
        if l == 0:
            wait_gather(reduce_gather(1, act, w_down.at[l], hid.at[0], None, hid.at[1]))
        else:
            gathers = reduce_gather(3, act, w_down.at[l], hid.at[2], None, fin.at[s])

    def place(g, i, u):
        first = pl.multiple_of(cols * i + width * u, width)
        for k in range(4):
            @pl.when(g == k)
            def _():
                for j in range(NUM_STEPS):
                    hid_v[j, 4 * k:4 * k + 4, pl.ds(first, width)] = fin[k, i, u, 4 * j:4 * j + 4]

    chunk_ids = (t,) + peer_t
    order = [(i, u) for u in range(SUB) for i in (0, 3, 2, 1)]
    fin_copies = []
    for i, u in order:
        if i == 3 and u == 0:
            order_rows(1)
            pltpu.make_async_copy(state_v, state_out, fin_sem.at[1]).start()

            @pl.when(s == 3)
            def _():
                pltpu.make_async_copy(rows_v, rows_out, fin_sem.at[2]).start()

        if i > 0:
            gathers[u][i - 1].wait_recv()
        chunk = fin.at[s, chunk_ids[i], u]
        fin_copies.append([send(chunk, chunk, fin_send.at[i, k, u], fin_recv.at[i, k, u], {"sp": flip_s[k]}) for k in (2, 1, 0)])
        place(s, chunk_ids[i], u)
    for n, (i, u) in enumerate(order):
        for k in range(3):
            fin_copies[n][k].wait_recv()
            place(flip_s[2 - k], chunk_ids[i], u)
    hid_copy = pltpu.make_async_copy(hid_v, hid_out, fin_sem.at[0])
    hid_copy.start()
    pltpu.make_async_copy(state_v, state_out, fin_sem.at[1]).wait()

    @pl.when(s == 3)
    def _():
        pltpu.make_async_copy(rows_v, rows_out, fin_sem.at[2]).wait()

    hid_copy.wait()
    for copy in sends:
        copy.wait_send()


def finish_kernel(hid_ref, state_ref, rows_ref, v_ref, z_ref, hid_out, state_out, vo_ref, zo_ref, hid, state, rows, in_sem, out_sem):
    last = lax.axis_index("sp") == 3
    hid_in = [pltpu.make_async_copy(hid_ref.at[j], hid.at[j], in_sem.at[j]) for j in range(NUM_STEPS)]
    hid_put = [pltpu.make_async_copy(hid.at[j], hid_out.at[j], out_sem.at[j]) for j in range(NUM_STEPS)]
    state_in = pltpu.make_async_copy(state_ref, state, in_sem.at[4])
    state_put = pltpu.make_async_copy(state, state_out, out_sem.at[4])
    rows_in = [pltpu.make_async_copy(rows_ref.at[a], rows.at[a], in_sem.at[5 + a]) for a in range(2)]
    rows_put = [pltpu.make_async_copy(rows.at[a], dst.at[:, :, pl.ds(0, 8)], out_sem.at[5 + a]) for a, dst in enumerate((vo_ref, zo_ref))]

    @pl.when(last)
    def _():
        for copy in rows_in:
            copy.start()

    for copy in [state_in] + hid_in:
        copy.start()

    @pl.when(last)
    def _():
        for before, after in zip(rows_in, rows_put):
            before.wait()
            after.start()

    for before, after in zip([state_in] + hid_in, [state_put] + hid_put):
        before.wait()
        after.start()
    for copy in [state_put] + hid_put:
        copy.wait()

    @pl.when(last)
    def _():
        for copy in rows_put:
            copy.wait()


def solution(mesh):
    sp_size = mesh.shape["sp"]

    def device_fn(step_emb, v_cache, z_cache, short_state, w_in, b_in, short_taps, long_filt, skip_gain, w_out, b_out, w_up, w_down):
        num_seq, shard_len, chan = v_cache.shape[1:]
        dim = step_emb.shape[-1]
        own = num_seq // sp_size
        rows = NUM_STEPS * own
        hbm = pl.BlockSpec(memory_space=pl.ANY)
        sds = jax.ShapeDtypeStruct

        v_out, z_out, part = pl.pallas_call(
            conv_kernel,
            name="conv_kernel",
            out_shape=(sds(v_cache.shape, BF16), sds(z_cache.shape, BF16), sds((2, sp_size, rows, chan), F32)),
            in_specs=[hbm] * 3,
            out_specs=(hbm, hbm, hbm),
            scratch_shapes=[
                pltpu.VMEM((16, own, shard_len, chan), BF16),
                pltpu.VMEM((2, shard_len + 8, chan), F32),
                pltpu.VMEM((NUM_STEPS, shard_len, chan), F32),
                pltpu.VMEM((2, sp_size, rows, chan), F32),
                pltpu.SemaphoreType.DMA((16,)),
                pltpu.SemaphoreType.DMA((16,)),
                pltpu.SemaphoreType.DMA((2,)),
                pltpu.SemaphoreType.DMA((2,)),
            ],
            compiler_params=pltpu.CompilerParams(vmem_limit_bytes=VMEM_LIMIT),
        )(v_cache, z_cache, long_filt)

        dma = pltpu.SemaphoreType.DMA
        chunk = (SUB, rows, chan // SUB)
        state_shape = sds((NUM_LAYERS, num_seq, 3, 2, chan), BF16)
        hid_shape = sds((NUM_STEPS, num_seq, dim), F32)
        rows_shape = sds((2, NUM_LAYERS, num_seq, 8, chan), BF16)
        hidden, states, new_rows = pl.pallas_call(
            dense_kernel,
            name="dense_kernel",
            out_shape=(hid_shape, state_shape, rows_shape),
            in_specs=[hbm] * 14,
            out_specs=(hbm, hbm, hbm),
            scratch_shapes=[
                pltpu.VMEM(step_emb.shape, BF16),
                pltpu.VMEM(state_shape.shape, BF16),
                pltpu.VMEM((3, NUM_LAYERS, chan), F32),
                pltpu.VMEM((3, 3, NUM_LAYERS, chan), F32),
                pltpu.VMEM((NUM_LAYERS, 2, chan), F32),
                pltpu.VMEM((NUM_LAYERS, dim), F32),
                pltpu.VMEM((2, 3, dim, chan), BF16),
                pltpu.VMEM((2, chan, dim), BF16),
                pltpu.VMEM((2, dim, w_up.shape[-1]), BF16),
                pltpu.VMEM((2, w_down.shape[1], dim), BF16),
                pltpu.VMEM((2, 2, 8, chan), F32),
                pltpu.VMEM((3, rows + 8, chan), F32),
                pltpu.VMEM((2 * rows, chan), F32),
                pltpu.VMEM((rows, dim), BF16),
                pltpu.VMEM((rows, w_up.shape[-1]), BF16),
                pltpu.VMEM((4,) + chunk, F32),
                pltpu.VMEM((4, own, shard_len, chan), BF16),
                pltpu.VMEM((2, shard_len + 8, chan), F32),
                pltpu.VMEM((NUM_STEPS, shard_len, chan), F32),
                pltpu.VMEM((4, sp_size, rows, chan), F32),
                pltpu.VMEM((4, 3, rows, chan), F32),
                pltpu.VMEM((4, 3) + chunk, F32),
                pltpu.VMEM((4, 3) + chunk, F32),
                pltpu.VMEM((3, 4) + chunk, F32),
                pltpu.VMEM((4, 4) + chunk, F32),
                pltpu.VMEM((4, 2, 56, chan), F32),
                pltpu.VMEM(hid_shape.shape, F32),
                pltpu.VMEM(state_shape.shape, BF16),
                pltpu.VMEM(rows_shape.shape, BF16),
                dma((2, 3)), dma(()), dma((2, 2)), dma((2, 4)), dma((2, 4)), dma(()), dma((8,)), dma((2,)), dma((3,)), dma((6,)),
                dma((4, 3)), dma((4, 3)), dma((4, 3, SUB)), dma((4, 3, SUB)), dma((4, 3, SUB)), dma((4, 3, SUB)), dma((4, 3, SUB)), dma((4, 3, SUB)),
                dma((2, 3)), dma((2, 3)),
            ],
            compiler_params=pltpu.CompilerParams(collective_id=0, has_side_effects=True, vmem_limit_bytes=VMEM_LIMIT),
        )(step_emb, jnp.transpose(short_state, (0, 1, 3, 2, 4)), jnp.transpose(b_in, (1, 0, 2)), jnp.transpose(short_taps, (1, 2, 0, 3)),
          skip_gain, b_out, part, v_cache, z_cache, long_filt, jnp.transpose(w_in, (0, 2, 1, 3)), w_out, w_up, w_down)

        hidden, states, v_out, z_out = pl.pallas_call(
            finish_kernel,
            name="finish_kernel",
            out_shape=(hid_shape, state_shape, sds(v_cache.shape, BF16), sds(z_cache.shape, BF16)),
            in_specs=[hbm] * 5,
            out_specs=(hbm,) * 4,
            input_output_aliases={3: 2, 4: 3},
            scratch_shapes=[pltpu.VMEM(hid_shape.shape, F32), pltpu.VMEM(state_shape.shape, BF16), pltpu.VMEM(rows_shape.shape, BF16),
                            dma((7,)), dma((7,))],
            compiler_params=pltpu.CompilerParams(vmem_limit_bytes=VMEM_LIMIT),
        )(hidden, states, new_rows, v_out, z_out)
        return (hidden, v_out, z_out, jnp.transpose(states, (0, 1, 3, 2, 4)))

    specs_in = (
        P(None, "dp", None),
        P(None, "dp", "sp", "tp"),
        P(None, "dp", "sp", "tp"),
        P(None, "dp", None, None, "tp"),
        P(None, None, None, "tp"),
        P(None, None, "tp"),
        P(None, None, None, "tp"),
        P(None, None, None, "tp"),
        P(None, None, "tp"),
        P(None, "tp", None),
        P(None, None),
        P(None, None, "tp"),
        P(None, "tp", None),
    )
    specs_out = (
        P(None, "dp", None),
        P(None, "dp", "sp", "tp"),
        P(None, "dp", "sp", "tp"),
        P(None, "dp", None, None, "tp"),
    )
    return jax.shard_map(device_fn, mesh=mesh, in_specs=specs_in, out_specs=specs_out, check_vma=False)
```

time: 75.4 us -> 72.8 us (0.966)
  Pallas kernels: 74.6 us -> 72 us
    pallas_call x2, Pallas kernels: 59.9 us -> 57.8 us  [the longest x1 55.9 us: device_fn(): pl.pallas_call(dense_kernel, name='dense_kernel', out_shape=(hid_shape, s...]
where the time goes in v4:
time: 72.8 us; the launch traced here: 72.7 us
  Pallas kernels  72 us (99%)
    pallas_call x1, Pallas kernels, device_fn(): pl.pallas_call(dense_kernel, name='dense_kernel', out_shape=(hid_shape, s...  55.9 us
    pallas_call x1, Pallas kernels, device_fn(): pl.pallas_call(conv_kernel, name='conv_kernel', out_shape=(sds(v_cache.sh...  14.2 us
    pallas_call x1, Pallas kernels, device_fn(): pl.pallas_call(finish_kernel, name='finish_kernel', out_shape=(hid_shape,...  1.99 us

profile of v4, /device:TPU:0, one launch (start us, length us, event | category | flops | bytes accessed | tf_op | source)
XLA Modules:
  0.0 72.7 jit_solution(7439517595626963262)
XLA Ops:
  0.6 14.2 %conv_kernel.1 = (bf16[2,16,256,512]{3,2,1,0:T(8,128)(2,1)}, bf16[2,16,256,512]{3,2,1,0:T(8,128)(2,1)}, f32[2,4,16,512]{3,2,1,0:T(8,128)}) custom-call(bf16[2,16,256,512]{3,2,1,0:T(8,128)(2,1)} %v_ref.3, bf16[2,16,256,512]{3,2,1,0:T(8,128)(2,1)} %z_ref.3, f32[2,2,1024,512]{3,2,1,0:T(8,128)} %f_ref.3), custom_call_target="tpu_custom_call" | custom-call | tf_op jit(solution)/shard_map/conv_kernel/pallas_call | solution.py:412
  14.8 55.9 %dense_kernel.1 = (f32[4,16,2048]{2,1,0:T(8,128)}, bf16[2,16,3,2,512]{4,3,2,1,0:T(2,128)(2,1)}, bf16[2,2,16,8,512]{4,3,2,1,0:T(8,128)(2,1)}) custom-call(bf16[4,16,2048]{2,1,0:T(8,128)(2,1)} %emb_hbm.1, bf16[2,16,3,2,512]{4,3,2,1,0:T(2,128)(2,1)} %bitcast.6, f32[3,2,512]{2,1,0:T(2,128)} %bitcast.8, f32[3,3,2,512]{3,2,1,0:T(2,128)} %bitcast.7, ...), custom_call_target="tpu_custom_call" | custom-call | tf_op jit(solution)/shard_map/dense_kernel/pallas_call | solution.py:436
  70.7 2.0 %finish_kernel.1 = (f32[4,16,2048]{2,1,0:T(8,128)}, bf16[2,16,3,2,512]{4,3,2,1,0:T(2,128)(2,1)}, bf16[2,16,256,512]{3,2,1,0:T(8,128)(2,1)}, bf16[2,16,256,512]{3,2,1,0:T(8,128)(2,1)}) custom-call(f32[4,16,2048]{2,1,0:T(8,128)} %get-tuple-element.15.hid_ref, ...), custom_call_target="tpu_custom_call", output_to_operand_aliasing={{2}: (3, {}), {3}: (4, {})} | custom-call | tf_op jit(solution)/shard_map/finish_kernel/pallas_call | solution.py:480

commit v5 on v4

--- a/solution.py
+++ b/solution.py
@@ -11,7 +11,7 @@
 F32 = jnp.float32
 BF16 = jnp.bfloat16
 VMEM_LIMIT = 66_500_000
-AHEAD = 8
+AHEAD = 10
 SUB = 1
 
 
@@ -129,15 +129,15 @@
         for copy in copies:
             copy.wait()
 
-    part_copy = pltpu.make_async_copy(part_hbm, part_ref.at[pl.ds(0, 2)], own_sem)
+    part_loads = [pltpu.make_async_copy(part_hbm.at[a], part_ref.at[a], own_sem.at[a]) for a in range(2)]
     shard_len = v_ref.shape[2]
     fwin_copies = [pltpu.make_async_copy(f_ref.at[1, a, pl.ds(window_base(shard_len), shard_len + 8)], fwin.at[a], fwin_sem.at[a])
                    for a in range(2)]
     reads = [pltpu.make_async_copy((v_ref, z_ref)[n // 4].at[1, pl.ds(4 * (n % 4), 4)], buf.at[n % 4], buf_sem.at[n]) for n in range(8)]
     small_copies = [pltpu.make_async_copy(src, dst, small_sem.at[i]) for i, (src, dst) in enumerate((
         (emb_hbm, emb_ref), (state_hbm, state_ref), (b_in_hbm, b_in_ref), (taps_hbm, taps_ref), (skip_hbm, skip_ref), (b_out_hbm, b_out_ref)))]
+    start(part_loads)
     start(small_copies)
-    part_copy.start()
     start(in_copies[0])
     lag_copy.start()
     start(out_copies[0])
@@ -146,8 +146,6 @@
     for k in range(3):
         pl.semaphore_signal(barrier, inc=1, device_id={"tp": flip_t[k]}, device_id_type=MESH)
         pl.semaphore_signal(barrier, inc=1, device_id={"sp": flip_s[k]}, device_id_type=MESH)
-    pl.semaphore_wait(barrier, 6)
-
     wait(small_copies)
     for k in range(4):
         @pl.when(s == k)
@@ -157,6 +155,7 @@
                     for u in range(SUB):
                         first = cols * i + width * u
                         emb[i, u, 4 * j:4 * j + 4] = emb_ref[j, :, first:first + width].astype(F32)[4 * k:4 * k + 4]
+    pl.semaphore_wait(barrier, 6)
 
     sends = []
 
@@ -167,8 +166,9 @@
         sends.append(copy)
         return copy
 
-    part_copy.wait()
     def send_part(a):
+        if a < 2:
+            part_loads[a].wait()
         return [send(part_ref.at[a, flip_s[k]], part_in.at[a, k], part_send.at[a, k], part_recv.at[a, k], {"sp": flip_s[k]})
                 for k in range(3)]
 
@@ -469,7 +469,7 @@
                 pltpu.VMEM(hid_shape.shape, F32),
                 pltpu.VMEM(state_shape.shape, BF16),
                 pltpu.VMEM(rows_shape.shape, BF16),
-                dma((2, 3)), dma(()), dma((2, 2)), dma((2, 4)), dma((2, 4)), dma(()), dma((8,)), dma((2,)), dma((3,)), dma((6,)),
+                dma((2, 3)), dma(()), dma((2, 2)), dma((2, 4)), dma((2, 4)), dma((2,)), dma((8,)), dma((2,)), dma((3,)), dma((6,)),
                 dma((4, 3)), dma((4, 3)), dma((4, 3, SUB)), dma((4, 3, SUB)), dma((4, 3, SUB)), dma((4, 3, SUB)), dma((4, 3, SUB)), dma((4, 3, SUB)),
                 dma((2, 3)), dma((2, 3)),
             ],

time: 72.8 us -> 72.3 us (level)
  no operation moved by 1% of the time
where the time goes in v5:
time: 72.3 us; the launch traced here: 72.1 us
  Pallas kernels  71.5 us (99%)
    pallas_call x1, Pallas kernels, device_fn(): pl.pallas_call(dense_kernel, name='dense_kernel', out_shape=(hid_shape, s...  55.4 us
    pallas_call x1, Pallas kernels, device_fn(): pl.pallas_call(conv_kernel, name='conv_kernel', out_shape=(sds(v_cache.sh...  14.1 us
    pallas_call x1, Pallas kernels, device_fn(): pl.pallas_call(finish_kernel, name='finish_kernel', out_shape=(hid_shape,...  1.99 us

profile of v5, /device:TPU:0, one launch (start us, length us, event | category | flops | bytes accessed | tf_op | source)
XLA Modules:
  0.0 72.1 jit_solution(10059011547606012864)
XLA Ops:
  0.6 14.1 %conv_kernel.1 = (bf16[2,16,256,512]{3,2,1,0:T(8,128)(2,1)}, bf16[2,16,256,512]{3,2,1,0:T(8,128)(2,1)}, f32[2,4,16,512]{3,2,1,0:T(8,128)}) custom-call(bf16[2,16,256,512]{3,2,1,0:T(8,128)(2,1)} %v_ref.3, bf16[2,16,256,512]{3,2,1,0:T(8,128)(2,1)} %z_ref.3, f32[2,2,1024,512]{3,2,1,0:T(8,128)} %f_ref.3), custom_call_target="tpu_custom_call" | custom-call | tf_op jit(solution)/shard_map/conv_kernel/pallas_call | solution.py:412
  14.8 55.4 %dense_kernel.1 = (f32[4,16,2048]{2,1,0:T(8,128)}, bf16[2,16,3,2,512]{4,3,2,1,0:T(2,128)(2,1)}, bf16[2,2,16,8,512]{4,3,2,1,0:T(8,128)(2,1)}) custom-call(bf16[4,16,2048]{2,1,0:T(8,128)(2,1)} %emb_hbm.1, bf16[2,16,3,2,512]{4,3,2,1,0:T(2,128)(2,1)} %bitcast.6, f32[3,2,512]{2,1,0:T(2,128)} %bitcast.8, f32[3,3,2,512]{3,2,1,0:T(2,128)} %bitcast.7, ...), custom_call_target="tpu_custom_call" | custom-call | tf_op jit(solution)/shard_map/dense_kernel/pallas_call | solution.py:436
  70.1 2.0 %finish_kernel.1 = (f32[4,16,2048]{2,1,0:T(8,128)}, bf16[2,16,3,2,512]{4,3,2,1,0:T(2,128)(2,1)}, bf16[2,16,256,512]{3,2,1,0:T(8,128)(2,1)}, bf16[2,16,256,512]{3,2,1,0:T(8,128)(2,1)}) custom-call(f32[4,16,2048]{2,1,0:T(8,128)} %get-tuple-element.15.hid_ref, ...), custom_call_target="tpu_custom_call", output_to_operand_aliasing={{2}: (3, {}), {3}: (4, {})} | custom-call | tf_op jit(solution)/shard_map/finish_kernel/pallas_call | solution.py:480

commit v6 on v5

--- a/solution.py
+++ b/solution.py
@@ -140,7 +140,6 @@
     start(small_copies)
     start(in_copies[0])
     lag_copy.start()
-    start(out_copies[0])
 
     barrier = pltpu.get_barrier_semaphore()
     for k in range(3):
@@ -263,6 +262,8 @@
         x = xrow[...]
         for g in range(3):
             in_copies[l][g].wait()
+            if l == 0 and g == 1:
+                start(out_copies[0])
             proj = jnp.dot(x, w_in[l, g], preferred_element_type=F32) + b_in_ref[g, l:l + 1]
             proj = proj.astype(BF16).astype(F32)
             ext[g, 8:24] = proj

time: 72.3 us -> 72.2 us (level)
  no operation moved by 1% of the time
where the time goes in v6:
time: 72.2 us; the launch traced here: 72 us
  Pallas kernels  71.4 us (99%)
    pallas_call x1, Pallas kernels, device_fn(): pl.pallas_call(dense_kernel, name='dense_kernel', out_shape=(hid_shape, s...  55.3 us
    pallas_call x1, Pallas kernels, device_fn(): pl.pallas_call(conv_kernel, name='conv_kernel', out_shape=(sds(v_cache.sh...  14.1 us
    pallas_call x1, Pallas kernels, device_fn(): pl.pallas_call(finish_kernel, name='finish_kernel', out_shape=(hid_shape,...  1.99 us

profile of v6, /device:TPU:0, one launch (start us, length us, event | category | flops | bytes accessed | tf_op | source)
XLA Modules:
  0.0 72.0 jit_solution(18308766216920365299)
XLA Ops:
  0.6 14.1 %conv_kernel.1 = (bf16[2,16,256,512]{3,2,1,0:T(8,128)(2,1)}, bf16[2,16,256,512]{3,2,1,0:T(8,128)(2,1)}, f32[2,4,16,512]{3,2,1,0:T(8,128)}) custom-call(bf16[2,16,256,512]{3,2,1,0:T(8,128)(2,1)} %v_ref.3, bf16[2,16,256,512]{3,2,1,0:T(8,128)(2,1)} %z_ref.3, f32[2,2,1024,512]{3,2,1,0:T(8,128)} %f_ref.3), custom_call_target="tpu_custom_call" | custom-call | tf_op jit(solution)/shard_map/conv_kernel/pallas_call | solution.py:413
  14.8 55.3 %dense_kernel.1 = (f32[4,16,2048]{2,1,0:T(8,128)}, bf16[2,16,3,2,512]{4,3,2,1,0:T(2,128)(2,1)}, bf16[2,2,16,8,512]{4,3,2,1,0:T(8,128)(2,1)}) custom-call(bf16[4,16,2048]{2,1,0:T(8,128)(2,1)} %emb_hbm.1, bf16[2,16,3,2,512]{4,3,2,1,0:T(2,128)(2,1)} %bitcast.6, f32[3,2,512]{2,1,0:T(2,128)} %bitcast.8, f32[3,3,2,512]{3,2,1,0:T(2,128)} %bitcast.7, ...), custom_call_target="tpu_custom_call" | custom-call | tf_op jit(solution)/shard_map/dense_kernel/pallas_call | solution.py:437
  70.1 2.0 %finish_kernel.1 = (f32[4,16,2048]{2,1,0:T(8,128)}, bf16[2,16,3,2,512]{4,3,2,1,0:T(2,128)(2,1)}, bf16[2,16,256,512]{3,2,1,0:T(8,128)(2,1)}, bf16[2,16,256,512]{3,2,1,0:T(8,128)(2,1)}) custom-call(f32[4,16,2048]{2,1,0:T(8,128)} %get-tuple-element.15.hid_ref, ...), custom_call_target="tpu_custom_call", output_to_operand_aliasing={{2}: (3, {}), {3}: (4, {})} | custom-call | tf_op jit(solution)/shard_map/finish_kernel/pallas_call | solution.py:481
